TPU v7x, 256 devices: a whole 4x4x8 slice. The times are simulated.
256 devices in a mesh: chan: 64 (over y, z, core), slot: 4 (over x).
Axes of the slice: x: 4, y: 4, z: 8, core: 2. Of those that a mesh axis runs over, the one named last changes fastest.
Arguments:
- visibility: float32 [2, 2, 256, 4, 3844], P(None, None, 'chan', 'slot'), parts along dimension 3, may hold values from -6 to 6
- coherency: bfloat16 [2, 2, 16, 256, 4, 3844], P(None, None, None, 'chan', 'slot'), parts along dimension 4, may hold values from -2 to 2
- jones_start: float32 [2, 2, 64, 256, 62], P(None, None, 'slot', 'chan'), parts along dimension 2, may hold values from -4 to 4
- duals_start: float32 [2, 2, 64, 256, 62], P(None, None, 'slot', 'chan'), parts along dimension 2, may hold values from -2 to 2
Outputs:
- jones_final: float32 [2, 2, 64, 256, 62], P(None, None, 'slot', 'chan'), parts along dimension 2
- consensus: float32 [2, 2, 64, 256, 62], P(None, None, 'slot', 'chan'), parts along dimension 2
- duals_final: float32 [2, 2, 64, 256, 62], P(None, None, 'slot', 'chan'), parts along dimension 2
- norms: float32 [8, 2], P('slot'), parts along dimension 0
There are 4 independent parts, one for each index of `slot`. A program takes and returns all parts, laid end to end along the dimension named above; each array names one. Nothing has to cross between parts.
All inputs are finite; a program needn't handle non-finite values.
Results may differ from a plain program's by a relative error of at most 0.0003.
Values sent between devices are 32-bit elements; how exact they have to be, the bound alone decides.
No kernel may reach another device: no remote copies, remote signals or barrier semaphores. Data moves between devices by JAX's collectives and lax.ppermute only.
A program may use at most 128 MiB of HBM per device.

v0:
```python
import jax
import jax.numpy as jnp
from jax import lax
from jax.sharding import PartitionSpec as P

ITERS = 2


penalty = 8.0
kernel_taps = (0.04, 0.06, 0.1, 0.15, 0.3, 0.15, 0.1, 0.06, 0.04)


def padded_2(block, sides, width):
    for axis, dim in sides:
        count = lax.axis_size(axis)
        forward = [(i, i + 1) for i in range(count - 1)]
        backward = [(target, source) for source, target in forward]
        low = lax.ppermute(
            lax.slice_in_dim(block, block.shape[dim] - width, None, axis=dim), axis, forward
        )
        high = lax.ppermute(lax.slice_in_dim(block, 0, width, axis=dim), axis, backward)
        block = jnp.concatenate([low, block, high], axis=dim)
    return block


def sent_to_all(x, axis):
    copies = jnp.broadcast_to(x, (lax.axis_size(axis), *x.shape))
    return lax.all_to_all(copies, axis, split_axis=0, concat_axis=0, tiled=True)


def taken_together(x, axis):
    everything = sent_to_all(x, axis)
    return jnp.sum(everything, axis=0)


def jones_update(visibility, coherency, jones_now, target):
    width = jones_now.shape[-1]
    grid_shape = coherency.shape[1:5] + (width, width)
    sky_real = coherency[0].astype(jnp.float32).reshape(grid_shape)
    sky_imag = coherency[1].astype(jnp.float32).reshape(grid_shape)
    vis_shape = visibility.shape[1:4] + (width, width)
    data_real = visibility[0].reshape(vis_shape)[:, None]
    data_imag = visibility[1].reshape(vis_shape)[:, None]
    left_real = jones_now[0][:, :, :, None, :, None]
    left_imag = jones_now[1][:, :, :, None, :, None]
    right_real = jones_now[0][:, :, :, None, None, :]
    right_imag = jones_now[1][:, :, :, None, None, :]
    crossed = 1.0 - jnp.eye(width, dtype=jnp.float32)
    half_real = left_real * sky_real - left_imag * sky_imag
    half_imag = left_real * sky_imag + left_imag * sky_real
    model_real = half_real * right_real + half_imag * right_imag
    model_imag = half_imag * right_real - half_real * right_imag
    rest_real = (data_real - jnp.sum(model_real, axis=1, keepdims=True) + model_real) * crossed
    rest_imag = (data_imag - jnp.sum(model_imag, axis=1, keepdims=True) + model_imag) * crossed
    weight_real = sky_real * right_real + sky_imag * right_imag
    weight_imag = sky_real * right_imag - sky_imag * right_real
    upper_real = jnp.sum(rest_real * weight_real - rest_imag * weight_imag, axis=(3, 5))
    upper_imag = jnp.sum(rest_real * weight_imag + rest_imag * weight_real, axis=(3, 5))
    lower = (
        jnp.sum(
            crossed
            * (sky_real * sky_real + sky_imag * sky_imag)
            * (right_real * right_real + right_imag * right_imag),
            axis=(3, 5),
        )
        + penalty
    )
    return jnp.stack(
        [(upper_real + penalty * target[0]) / lower, (upper_imag + penalty * target[1]) / lower]
    )


def smooth(padded, channels):
    total = kernel_taps[0] * padded[:, :, :, 0:channels]
    for offset in range(1, 9):
        total = total + kernel_taps[offset] * padded[:, :, :, offset : offset + channels]
    return total


def local(visibility, coherency, jones_start, duals_start):
    channels = jones_start.shape[3]
    entries = jones_start.size * lax.axis_size("chan")
    jones_now = jones_start
    consensus = jones_start
    duals_now = duals_start
    partials = []
    for iteration in range(ITERS):
        jones_now = jones_update(visibility, coherency, jones_now, consensus - duals_now)
        padded = padded_2(jones_now + duals_now, (("chan", 3),), 4)
        fresh = smooth(padded, channels)
        duals_now = duals_now + jones_now - fresh
        primal_gap = jones_now - fresh
        moved = fresh - consensus
        pieces = (jnp.sum(primal_gap * primal_gap), penalty * penalty * jnp.sum(moved * moved))
        partials.append(jnp.stack([pieces[0], pieces[1]]))
        consensus = fresh
    norms = taken_together(jnp.stack(partials), "chan") / entries
    return (jones_now, consensus, duals_now, norms)


def solution(mesh):
    placed = (
        P(None, None, "chan", "slot", None),
        P(None, None, None, "chan", "slot", None),
        P(None, None, "slot", "chan", None),
        P(None, None, "slot", "chan", None),
    )
    return jax.shard_map(
        local,
        mesh=mesh,
        in_specs=placed,
        out_specs=(
            P(None, None, "slot", "chan", None),
            P(None, None, "slot", "chan", None),
            P(None, None, "slot", "chan", None),
            P("slot", None),
        ),
        check_vma=False,
    )
```

profile of v0, /device:TPU:1, one launch (start us, length us, event | category | flops | bytes accessed | tf_op | source)
XLA Modules:
  0.0 159.5 jit_solution(7662246619976627062)
XLA Ops:
  1.5 1.5 multiply_add_fusion.7
  3.1 2.5 %mul.1257 = f32[2,16,4,62,62]{4,3,1,2,0:T(8,128)} broadcast(f32[2,16,4,62]{3,1,2,0:T(8,128)S(1)} %copy.64), dimensions={0,1,2,3} | broadcast | bytes 1999872 | tf_op jit(solution)/shard_map/mul | solution.py:49
  5.6 5.0 %mul.1258 = f32[1,2,16,4,1,3844]{5,2,3,1,4,0:T(8,128)} reshape(f32[2,16,4,62,62]{4,3,1,2,0:T(8,128)} %mul.1257) | data formatting | bytes 3936256 | tf_op jit(solution)/shard_map/mul | solution.py:49
  10.6 2.5 %mul.1261 = f32[2,16,4,62,62]{4,3,1,2,0:T(8,128)} broadcast(f32[2,16,4,62]{3,1,2,0:T(8,128)S(1)} %copy.66), dimensions={0,1,2,3} | broadcast | bytes 1999872 | tf_op jit(solution)/shard_map/mul | solution.py:49
  13.1 5.0 %mul.1262 = f32[1,2,16,4,1,3844]{5,2,3,1,4,0:T(8,128)} reshape(f32[2,16,4,62,62]{4,3,1,2,0:T(8,128)} %mul.1261) | data formatting | bytes 3936256 | tf_op jit(solution)/shard_map/mul | solution.py:49
  18.1 2.2 %mul.1264 = f32[2,16,4,62,62]{4,3,1,2,0:T(8,128)} broadcast(f32[2,16,4,62]{3,1,2,0:T(8,128)S(1)} %copy.64), dimensions={0,1,2,4} | broadcast | bytes 1999872 | tf_op jit(solution)/shard_map/mul | solution.py:51
  20.3 5.0 %mul.1265 = f32[1,2,16,4,1,3844]{5,2,3,1,4,0:T(8,128)} reshape(f32[2,16,4,62,62]{4,3,1,2,0:T(8,128)} %mul.1264) | data formatting | bytes 3936256 | tf_op jit(solution)/shard_map/mul | solution.py:51
  25.3 2.2 %mul.1269 = f32[2,16,4,62,62]{4,3,1,2,0:T(8,128)} broadcast(f32[2,16,4,62]{3,1,2,0:T(8,128)S(1)} %copy.66), dimensions={0,1,2,4} | broadcast | bytes 1999872 | tf_op jit(solution)/shard_map/mul | solution.py:51
  27.5 5.0 %mul.1270 = f32[1,2,16,4,1,3844]{5,2,3,1,4,0:T(8,128)} reshape(f32[2,16,4,62,62]{4,3,1,2,0:T(8,128)} %mul.1269) | data formatting | bytes 3936256 | tf_op jit(solution)/shard_map/mul | solution.py:51
  32.5 2.4 %fusion.49 = (bf16[1,2,16,4,1,3844]{5,3,4,2,1,0:T(4,128)(2,1)S(1)}, bf16[1,2,16,4,1,3844]{5,3,4,2,1,0:T(4,128)(2,1)S(1)}) fusion(bf16[2,2,16,4,1,3844]{5,3,4,2,1,0:T(4,128)(2,1)} %param.5), kind=kLoop, calls=%fused_computation.123 | loop fusion | bytes 3936256 | tf_op jit(solution)/shard_map/slice | solution.py:39
  34.9 2.3 %copy_convert_fusion = (f32[1,2,16,4,1,3844]{5,2,3,1,4,0:T(8,128)}, f32[1,2,16,4,1,3844]{5,2,3,1,4,0:T(8,128)}) fusion(bf16[1,2,16,4,1,3844]{5,3,4,2,1,0:T(4,128)(2,1)S(1)} %get-tuple-element.40, bf16[1,2,16,4,1,3844]{5,3,4,2,1,0:T(4,128)(2,1)S(1)} %get-tuple-element.39), kind=kLoop, calls=%fused_computation.27 | loop fusion | flops 984064 | bytes 5904384 | tf_op jit(solution)/shard_map/convert_element_type | solution.py:40
  37.2 1.6 %subtract_reduce_fusion.3 = (f32[2,4,3844]{2,1,0:T(4,128)S(1)}, f32[2,4,3844]{2,1,0:T(4,128)S(1)}) fusion(f32[1,2,16,4,1,3844]{5,2,3,1,4,0:T(8,128)S(1)} %copy-done.3, f32[1,2,16,4,1,3844]{5,2,3,1,4,0:T(8,128)S(1)} %copy-done.2, f32[1,2,16,4,1,3844]{5,2,3,1,4,0:T(8,128)S(1)} %copy-done.1, bf16[1,2,16,4,1,3844]{5,3,4,2,1,0:T(4,128)(2,1)S(1)} %get-tuple-element.40, ...), kind=kLoop, calls=%fused_computation.23 | loop fusion | flops 7811008 | bytes 10086656 | tf_op jit(solution)/shard_map/reduce_sum | solution.py:54
  41.0 8.4 %reshape.965 = f32[2,16,4,1,62,62]{5,4,1,2,0,3:T(8,128)} reshape(f32[1,2,16,4,1,3844]{5,2,3,1,4,0:T(8,128)} %get-tuple-element.49) | data formatting | bytes 3936256 | tf_op jit(solution)/shard_map/convert_element_type | solution.py:39
  49.4 8.2 %reshape.966 = f32[2,16,4,1,62,62]{5,4,1,2,0,3:T(8,128)} reshape(f32[1,2,16,4,1,3844]{5,2,3,1,4,0:T(8,128)} %get-tuple-element.48) | data formatting | bytes 3936256 | tf_op jit(solution)/shard_map/convert_element_type | solution.py:40
  58.5 10.0 %subtract_reduce_fusion.1 = (f32[2,16,4,62]{3,1,2,0:T(8,128)S(1)}, f32[2,16,4,62]{3,1,2,0:T(8,128)S(1)}, f32[2,16,4,62]{3,1,2,0:T(8,128)S(1)}) fusion(f32[2,16,4,1,62,62]{5,4,1,2,0,3:T(8,128)} %reshape.966, f32[2,16,4,62]{3,1,2,0:T(8,128)S(1)} %copy.66, f32[2,16,4,1,62,62]{5,4,1,2,0,3:T(8,128)} %reshape.965, f32[2,16,4,62]{3,1,2,0:T(8,128)S(1)} %copy.64, ...), kind=kLoop, calls=%fused_computation.12 | loop fusion | flops 17689344 | bytes 4388112 | tf_op jit(solution)/shard_map/reduce_sum | solution.py:57
  68.6 4.9 %collective-permute-start = (f32[2,2,16,4,62]{4,2,3,1,0:T(8,128)S(1)}, f32[2,2,16,4,62]{4,2,3,1,0:T(8,128)}, u32[]{:S(2)}, u32[]{:S(2)}) collective-permute-start(f32[2,2,16,4,62]{4,2,3,1,0:T(8,128)S(1)} %copy_add_fusion), channel_id=1, source_target_pairs={{0,4},{4,8},{8,12},{12,16},{16,20},{20,24},{24,28},{28,32},{32,36}... | collective-permute-start | bytes 190472 | tf_op jit(solution)/shard_map/ppermute | solution.py:18
  73.5 2.1 %collective-permute-start.1 = (f32[2,2,16,4,62]{4,2,3,1,0:T(8,128)S(1)}, f32[2,2,16,4,62]{4,2,3,1,0:T(8,128)}, u32[]{:S(2)}, u32[]{:S(2)}) collective-permute-start(f32[2,2,16,4,62]{4,2,3,1,0:T(8,128)S(1)} %copy_add_fusion), channel_id=1, source_target_pairs={{4,0},{8,4},{12,8},{16,12},{20,16},{24,20},{28,24},{32,28},{36,32}... | collective-permute-start | bytes 190472 | tf_op jit(solution)/shard_map/ppermute | solution.py:21
  75.7 2.6 %mul.1304 = f32[2,16,4,62,62]{4,3,1,2,0:T(8,128)} broadcast(f32[2,16,4,62]{3,1,2,0:T(8,128)S(1)} %get-tuple-element.34), dimensions={0,1,2,3} | broadcast | bytes 1999872 | tf_op jit(solution)/shard_map/mul | solution.py:49
  78.3 5.0 %mul.1305 = f32[1,2,16,4,1,3844]{5,2,3,1,4,0:T(8,128)} reshape(f32[2,16,4,62,62]{4,3,1,2,0:T(8,128)} %mul.1304) | data formatting | bytes 3936256 | tf_op jit(solution)/shard_map/mul | solution.py:49
  83.3 2.6 %mul.1311 = f32[2,16,4,62,62]{4,3,1,2,0:T(8,128)} broadcast(f32[2,16,4,62]{3,1,2,0:T(8,128)S(1)} %get-tuple-element.35), dimensions={0,1,2,3} | broadcast | bytes 1999872 | tf_op jit(solution)/shard_map/mul | solution.py:49
  85.8 5.0 %mul.1312 = f32[1,2,16,4,1,3844]{5,2,3,1,4,0:T(8,128)} reshape(f32[2,16,4,62,62]{4,3,1,2,0:T(8,128)} %mul.1311) | data formatting | bytes 3936256 | tf_op jit(solution)/shard_map/mul | solution.py:49
  90.8 2.2 %mul.1314 = f32[2,16,4,62,62]{4,3,1,2,0:T(8,128)} broadcast(f32[2,16,4,62]{3,1,2,0:T(8,128)S(1)} %get-tuple-element.34), dimensions={0,1,2,4} | broadcast | bytes 1999872 | tf_op jit(solution)/shard_map/mul | solution.py:51
  93.1 5.0 %mul.1315 = f32[1,2,16,4,1,3844]{5,2,3,1,4,0:T(8,128)} reshape(f32[2,16,4,62,62]{4,3,1,2,0:T(8,128)} %mul.1314) | data formatting | bytes 3936256 | tf_op jit(solution)/shard_map/mul | solution.py:51
  98.1 2.2 %mul.1319 = f32[2,16,4,62,62]{4,3,1,2,0:T(8,128)} broadcast(f32[2,16,4,62]{3,1,2,0:T(8,128)S(1)} %get-tuple-element.35), dimensions={0,1,2,4} | broadcast | bytes 1999872 | tf_op jit(solution)/shard_map/mul | solution.py:51
  100.3 5.0 %mul.1320 = f32[1,2,16,4,1,3844]{5,2,3,1,4,0:T(8,128)} reshape(f32[2,16,4,62,62]{4,3,1,2,0:T(8,128)} %mul.1319) | data formatting | bytes 3936256 | tf_op jit(solution)/shard_map/mul | solution.py:51
  105.3 4.9 %subtract_reduce_fusion.2 = (f32[2,4,3844]{2,1,0:T(4,128)S(1)}, f32[2,4,3844]{2,1,0:T(4,128)S(1)}) fusion(f32[1,2,16,4,1,3844]{5,2,3,1,4,0:T(8,128)} %mul.1320, f32[1,2,16,4,1,3844]{5,2,3,1,4,0:T(8,128)} %mul.1315, f32[1,2,16,4,1,3844]{5,2,3,1,4,0:T(8,128)} %mul.1312, bf16[1,2,16,4,1,3844]{5,3,4,2,1,0:T(4,128)(2,1)S(1)} %get-tuple-element.40, ...), kind=kLoop, calls=%fused_computation.19 | loop fusion | flops 7811008 | bytes 10086656 | tf_op jit(solution)/shard_map/reduce_sum | solution.py:54
  111.0 10.0 %subtract_reduce_fusion = (f32[2,16,4,62]{3,1,2,0:T(8,128)S(1)}, f32[2,16,4,62]{3,1,2,0:T(8,128)S(1)}, f32[2,16,4,62]{3,1,2,0:T(8,128)S(1)}) fusion(f32[2,16,4,1,62,62]{5,4,1,2,0,3:T(8,128)} %reshape.966, f32[2,16,4,62]{3,1,2,0:T(8,128)S(1)} %get-tuple-element.35, f32[2,16,4,1,62,62]{5,4,1,2,0,3:T(8,128)} %reshape.965, ...), kind=kLoop, calls=%fused_computation.2 | loop fusion | flops 17689344 | bytes 4388112 | tf_op jit(solution)/shard_map/reduce_sum | solution.py:57
  122.3 3.4 %collective-permute-start.2 = (f32[2,2,16,4,62]{4,2,3,1,0:T(8,128)S(1)}, f32[2,2,16,4,62]{4,2,3,1,0:T(8,128)S(1)}, u32[]{:S(2)}, u32[]{:S(2)}) collective-permute-start(f32[2,2,16,4,62]{4,2,3,1,0:T(8,128)S(1)} %fusion.43), channel_id=1, source_target_pairs={{0,4},{4,8},{8,12},{12,16},{16,20},{20,24},{24,28},{28,32},{32,36}... | collective-permute-start | bytes 190472 | tf_op jit(solution)/shard_map/ppermute | solution.py:18
  125.8 1.9 %collective-permute-start.3 = (f32[2,2,16,4,62]{4,2,3,1,0:T(8,128)S(1)}, f32[2,2,16,4,62]{4,2,3,1,0:T(8,128)S(1)}, u32[]{:S(2)}, u32[]{:S(2)}) collective-permute-start(f32[2,2,16,4,62]{4,2,3,1,0:T(8,128)S(1)} %fusion.43), channel_id=1, source_target_pairs={{4,0},{8,4},{12,8},{16,12},{20,16},{24,20},{28,24},{32,28},{36,32}... | collective-permute-start | bytes 190472 | tf_op jit(solution)/shard_map/ppermute | solution.py:21
  127.7 4.3 %collective-permute-done.3 = f32[2,2,16,4,62]{4,2,3,1,0:T(8,128)S(1)} collective-permute-done((f32[2,2,16,4,62]{4,2,3,1,0:T(8,128)S(1)}, f32[2,2,16,4,62]{4,2,3,1,0:T(8,128)S(1)}, u32[]{:S(2)}, u32[]{:S(2)}) %collective-permute-start.3) | collective-permute-done | bytes 63520 | tf_op jit(solution)/shard_map/ppermute | solution.py:21
  136.3 12.8 %all-to-all-start = ((f32[64,2,2]{2,1,0:T(2,128)}), f32[64,2,2]{2,1,0:T(2,128)S(1)}, u32[]{:S(2)}, u32[]{:S(2)}) async-start(f32[64,2,2]{2,1,0:T(2,128)} %broadcast_in_dim.25), calls=%async_computation | async-start | bytes 131072 | tf_op jit(solution)/shard_map/all_to_all | solution.py:28
  151.3 7.6 %all-to-all-done = f32[64,2,2]{2,1,0:T(2,128)S(1)} async-done(((f32[64,2,2]{2,1,0:T(2,128)}), f32[64,2,2]{2,1,0:T(2,128)S(1)}, u32[]{:S(2)}, u32[]{:S(2)}) %all-to-all-start) | async-done | bytes 1056 | tf_op jit(solution)/shard_map/all_to_all | solution.py:28
  (51 shorter events, 11.8 us)
Async XLA Ops:
  32.5 4.7 %copy-start = (f32[1,2,16,4,1,3844]{5,2,3,1,4,0:T(8,128)S(1)}, f32[1,2,16,4,1,3844]{5,2,3,1,4,0:T(8,128)}, u32[]{:S(2)}) copy-start(f32[1,2,16,4,1,3844]{5,2,3,1,4,0:T(8,128)} %mul.1258) | copy-start | bytes 5904388
  32.5 4.7 %copy-start.1 = (f32[1,2,16,4,1,3844]{5,2,3,1,4,0:T(8,128)S(1)}, f32[1,2,16,4,1,3844]{5,2,3,1,4,0:T(8,128)}, u32[]{:S(2)}) copy-start(f32[1,2,16,4,1,3844]{5,2,3,1,4,0:T(8,128)} %mul.1262) | copy-start | bytes 5904388
  32.5 4.7 %copy-start.2 = (f32[1,2,16,4,1,3844]{5,2,3,1,4,0:T(8,128)S(1)}, f32[1,2,16,4,1,3844]{5,2,3,1,4,0:T(8,128)}, u32[]{:S(2)}) copy-start(f32[1,2,16,4,1,3844]{5,2,3,1,4,0:T(8,128)} %mul.1265) | copy-start | bytes 5904388
  32.5 4.7 %copy-start.3 = (f32[1,2,16,4,1,3844]{5,2,3,1,4,0:T(8,128)S(1)}, f32[1,2,16,4,1,3844]{5,2,3,1,4,0:T(8,128)}, u32[]{:S(2)}) copy-start(f32[1,2,16,4,1,3844]{5,2,3,1,4,0:T(8,128)} %mul.1270) | copy-start | bytes 5904388
  37.2 2.0 %copy-start.6 = (f32[2,2,4,1,3844]{4,3,2,1,0:T(1,128)S(1)}, f32[2,2,4,1,3844]{4,3,2,1,0:T(1,128)}, u32[]{:S(2)}) copy-start(f32[2,2,4,1,3844]{4,3,2,1,0:T(1,128)} %param.4) | copy-start | bytes 738052
  49.3 9.1 %copy-start.4 = (f32[2,2,16,4,62]{4,3,2,1,0:T(4,128)S(1)}, f32[2,2,16,4,62]{4,3,2,1,0:T(4,128)}, u32[]{:S(2)}) copy-start(f32[2,2,16,4,62]{4,3,2,1,0:T(4,128)} %param.6) | copy-start | bytes 190468
  49.4 9.1 %copy-start.5 = (f32[2,2,16,4,62]{4,3,2,1,0:T(4,128)S(1)}, f32[2,2,16,4,62]{4,3,2,1,0:T(4,128)}, u32[]{:S(2)}) copy-start(f32[2,2,16,4,62]{4,3,2,1,0:T(4,128)} %param.7) | copy-start | bytes 190468
  68.6 52.4 %collective-permute-start = (f32[2,2,16,4,62]{4,2,3,1,0:T(8,128)S(1)}, f32[2,2,16,4,62]{4,2,3,1,0:T(8,128)}, u32[]{:S(2)}, u32[]{:S(2)}) collective-permute-start(f32[2,2,16,4,62]{4,2,3,1,0:T(8,128)S(1)} %copy_add_fusion), channel_id=1, source_target_pairs={{0,4},{4,8},{8,12},{12,16},{16,20},{20,24},{24,28},{28,32},{32,36}... | collective-permute-start | bytes 190472 | tf_op jit(solution)/shard_map/ppermute | solution.py:18
  73.5 47.5 %collective-permute-start.1 = (f32[2,2,16,4,62]{4,2,3,1,0:T(8,128)S(1)}, f32[2,2,16,4,62]{4,2,3,1,0:T(8,128)}, u32[]{:S(2)}, u32[]{:S(2)}) collective-permute-start(f32[2,2,16,4,62]{4,2,3,1,0:T(8,128)S(1)} %copy_add_fusion), channel_id=1, source_target_pairs={{4,0},{8,4},{12,8},{16,12},{20,16},{24,20},{28,24},{32,28},{36,32}... | collective-permute-start | bytes 190472 | tf_op jit(solution)/shard_map/ppermute | solution.py:21
  122.3 5.4 %collective-permute-start.2 = (f32[2,2,16,4,62]{4,2,3,1,0:T(8,128)S(1)}, f32[2,2,16,4,62]{4,2,3,1,0:T(8,128)S(1)}, u32[]{:S(2)}, u32[]{:S(2)}) collective-permute-start(f32[2,2,16,4,62]{4,2,3,1,0:T(8,128)S(1)} %fusion.43), channel_id=1, source_target_pairs={{0,4},{4,8},{8,12},{12,16},{16,20},{20,24},{24,28},{28,32},{32,36}... | collective-permute-start | bytes 190472 | tf_op jit(solution)/shard_map/ppermute | solution.py:18
  125.8 6.3 %collective-permute-start.3 = (f32[2,2,16,4,62]{4,2,3,1,0:T(8,128)S(1)}, f32[2,2,16,4,62]{4,2,3,1,0:T(8,128)S(1)}, u32[]{:S(2)}, u32[]{:S(2)}) collective-permute-start(f32[2,2,16,4,62]{4,2,3,1,0:T(8,128)S(1)} %fusion.43), channel_id=1, source_target_pairs={{4,0},{8,4},{12,8},{16,12},{20,16},{24,20},{28,24},{32,28},{36,32}... | collective-permute-start | bytes 190472 | tf_op jit(solution)/shard_map/ppermute | solution.py:21
  136.3 22.6 %all-to-all-start = ((f32[64,2,2]{2,1,0:T(2,128)}), f32[64,2,2]{2,1,0:T(2,128)S(1)}, u32[]{:S(2)}, u32[]{:S(2)}) async-start(f32[64,2,2]{2,1,0:T(2,128)} %broadcast_in_dim.25), calls=%async_computation | async-start | bytes 131072 | tf_op jit(solution)/shard_map/all_to_all | solution.py:28
where the time goes:
time: 161 us; the launch traced here: 160 us
  local copies, waits for them, and re-layouts  85.3 us (53%)
  other arithmetic  34.8 us (22%)
  starting transfers between devices  25.2 us (16%)
  waiting for transfers between devices  12 us (7%)
  between operations  2.22 us (1%)
    mul x11, local copies, waits for them, and re-layouts, jones_update(): half_real = left_real * sky_real - left_imag * sky_imag  31.1 us
    mul x8, local copies, waits for them, and re-layouts, jones_update(): model_real = half_real * right_real + half_imag * right_imag  28.8 us
    reduce_sum x2, other arithmetic, jones_update(): jnp.sum(rest_real * weight_real - rest_imag * weight_imag, axis=(3, 5))  19.9 us
    all_to_all x1, starting transfers between devices, sent_to_all(): return lax.all_to_all(copies, axis, split_axis=0, concat_axis=0, tiled=True)  12.8 us
    convert_element_type x1, local copies, waits for them, and re-layouts, jones_update(): sky_real = coherency[0].astype(jnp.float32).reshape(grid_shape)  8.38 us
    ppermute x2, starting transfers between devices, padded_2(): lax.ppermute(lax.slice_in_dim(block, block.shape[dim] - width, None, axis...  8.37 us
    convert_element_type x1, local copies, waits for them, and re-layouts, jones_update(): sky_imag = coherency[1].astype(jnp.float32).reshape(grid_shape)  8.23 us
    all_to_all x1, waiting for transfers between devices, sent_to_all(): return lax.all_to_all(copies, axis, split_axis=0, concat_axis=0, tiled=True)  7.62 us
  transfers between devices with their start and end apart: 5, of which 2 were waited for; matrix products, arithmetic and copies ran while one was open for 30% of the time, Pallas kernels for 0%

commit v1 on v0

v1 whole, which is shorter than its diff:
```python
import jax
import jax.numpy as jnp
from jax import lax
from jax.experimental import pallas as pl
from jax.experimental.pallas import tpu as pltpu
from jax.sharding import PartitionSpec as P

penalty = 8.0
kernel_taps = (0.04, 0.06, 0.1, 0.15, 0.3, 0.15, 0.1, 0.06, 0.04)
N = 62
M = 64
LANES = 128
PAIRS = N * N
F32 = jnp.float32
BF16 = jnp.bfloat16
GROUP = 4


def iota(shape, dim):
    return lax.broadcasted_iota(jnp.int32, shape, dim)


def rows_first(ref, out_rows=M):
    halves = []
    for part in range(2):
        x = jnp.concatenate([ref[part, pol, k] for pol in range(2) for k in range(16)], axis=0)
        x = jnp.concatenate([x, jnp.zeros((LANES, LANES - N), F32)], axis=1)
        halves.append(x.T[:out_rows])
    return jnp.concatenate(halves, axis=1)


def rows_last(x, ref):
    for part in range(2):
        half = x[:, part * LANES : (part + 1) * LANES]
        half = jnp.concatenate([half, jnp.zeros((LANES - M, LANES), F32)], axis=0).T
        for pol in range(2):
            for k in range(16):
                at = (pol * 16 + k) * 4
                ref[part, pol, k] = half[at : at + 4, :N]


def lay_out(coh_ref, vis_ref, flat, vflat, ct, vt):
    width = 31 * LANES
    flat[:, width - LANES :] = jnp.zeros((256, LANES), BF16)
    vflat[:, width - LANES :] = jnp.zeros((48, LANES), BF16)
    for part in range(2):
        for pol in range(2):
            for k in range(0, 16, 4):
                at = part * 128 + pol * 64 + k * 4
                block = [coh_ref[part, pol, k + i].astype(F32) for i in range(4)]
                flat[at : at + 16, :PAIRS] = jnp.concatenate(block, axis=0).astype(BF16)
    v = jnp.concatenate([vis_ref[part, pol] for part in range(2) for pol in range(2)], axis=0)
    for split in range(3):
        high = v.astype(BF16)
        vflat[split * 16 : split * 16 + 16, :PAIRS] = high
        v = v - high.astype(F32)
    row = iota((128, 256), 0)
    col = iota((128, 256), 1)
    half = row // M
    q = row % M
    lag = jnp.where(q < N, col - half * N - q, 1000)
    own = q - half
    source = iota((48, 256), 0)
    target = iota((48, 256), 1)
    spread = (
        ((source % 16) // 8 == target // LANES)
        & ((source % 8) // 4 == (target % LANES) // 64)
        & (source % 4 == target % 4)
    )
    spread = jnp.where(spread, 1.0, 0.0).astype(BF16)
    for t in range(31):
        start = 124 * t // LANES * LANES
        shift = 124 * t - start
        pick = jnp.where((lag == shift) & (own != 2 * t), 1.0, 0.0).astype(BF16)
        contract = (((1,), (1,)), ((), ()))
        ct[t * 128 : t * 128 + 128] = lax.dot_general(
            pick, flat[:, start : start + 256], contract, preferred_element_type=F32
        )
        short = lax.dot_general(
            pick, vflat[:, start : start + 256], contract, preferred_element_type=F32
        )
        vt[t * 128 : t * 128 + 128] = jnp.dot(
            short.astype(BF16), spread, preferred_element_type=F32
        )
    ct[31 * 128 :] = jnp.zeros((128, 256), F32)
    vt[31 * 128 :] = jnp.zeros((128, 256), F32)


def pair_sums(ct, vt, gain, total, weight, lhs, half, model):
    row = iota((256, LANES), 0) % LANES
    col = iota((256, LANES), 1)
    same = (row // 64 == col // 64) & (row % 4 == col % 4)
    adder = jnp.where(same, 1.0, 0.0).astype(BF16)

    def front(group):
        slot = group % 2
        for i in range(GROUP):
            p = group * GROUP + i
            c_real = ct[p * M : p * M + M, :LANES]
            c_imag = ct[p * M : p * M + M, LANES:]
            q_real = gain[:, :LANES]
            q_imag = gain[:, LANES:]
            h_real = c_real * q_real + c_imag * q_imag
            h_imag = c_imag * q_real - c_real * q_imag
            p_real = gain[p : p + 1, :LANES]
            p_imag = gain[p : p + 1, LANES:]
            half[slot, i * M : i * M + M, :LANES] = h_real
            half[slot, i * M : i * M + M, LANES:] = h_imag
            for at, m in (
                (i * 128, p_real * h_real - p_imag * h_imag),
                (i * 128 + M, p_real * h_imag + p_imag * h_real),
            ):
                high = m.astype(BF16)
                lhs[slot, at : at + M, :LANES] = high
                lhs[slot, at : at + M, LANES:] = (m - high.astype(F32)).astype(BF16)
        model[slot] = jnp.dot(lhs[slot], adder, preferred_element_type=F32)

    def back(group):
        slot = group % 2
        for i in range(GROUP):
            p = group * GROUP + i
            h_real = half[slot, i * M : i * M + M, :LANES]
            h_imag = half[slot, i * M : i * M + M, LANES:]
            d_real = vt[p * M : p * M + M, :LANES] - model[slot, i * 128 : i * 128 + M]
            d_imag = vt[p * M : p * M + M, LANES:] - model[slot, i * 128 + M : i * 128 + 128]

            def over_q(x):
                return jnp.sum(x, axis=0, keepdims=True)

            total[p : p + 1, :LANES] = over_q(d_real * h_real + d_imag * h_imag)
            total[p : p + 1, LANES:] = over_q(d_imag * h_real - d_real * h_imag)
            weight[p : p + 1] = over_q(h_real * h_real + h_imag * h_imag)

    front(0)
    for group in range(M // GROUP):
        if group + 1 < M // GROUP:
            front(group + 1)
        back(group)


def solved(total, weight, gain, target):
    twice = jnp.concatenate([weight, weight], axis=1)
    return (total + gain * twice + penalty * target) / (twice + penalty)


def first_kernel(
    coh_ref, vis_ref, jones_ref, duals_ref,
    sum_ref, gain_ref, start_ref, duals_out, ct, vt,
    flat, vflat, total, weight, lhs, half, model,
):
    lay_out(coh_ref, vis_ref, flat, vflat, ct, vt)
    start_ref[...] = rows_first(jones_ref)
    duals_out[...] = rows_first(duals_ref)
    pair_sums(ct, vt, start_ref, total, weight, lhs, half, model)
    gain = solved(total[...], weight[...], start_ref[...], start_ref[...] - duals_out[...])
    gain_ref[...] = gain
    sum_ref[...] = gain + duals_out[...]


def second_kernel(ct, vt, gain_ref, total, weight, lhs, half, model):
    pair_sums(ct, vt, gain_ref, total, weight, lhs, half, model)


def smoothed(odd, own, inner, outer):
    source = iota((LANES, LANES), 0)
    target = iota((LANES, LANES), 1)
    lag = jnp.where(source // 4 == target // 4, source % 4 - target % 4, 100)

    def taps(shift):
        out = jnp.zeros((LANES, LANES), F32)
        for offset in range(-4, 5):
            out = jnp.where(lag + shift == offset, kernel_taps[offset + 4], out)
        return out

    after, before = taps(4), taps(-4)
    weights = jnp.concatenate(
        [taps(0), jnp.where(odd, before, after), jnp.where(odd, after, before)], axis=0
    )
    halves = []
    for part in range(2):
        x = jnp.concatenate(
            [a[:, part * LANES : (part + 1) * LANES] for a in (own, inner, outer)], axis=1
        )
        halves.append(
            jnp.dot(x, weights, precision=lax.Precision.HIGHEST, preferred_element_type=F32)
        )
    return jnp.concatenate(halves, axis=1)


def gaps(gain, fresh, consensus):
    primal = gain - fresh
    moved = fresh - consensus
    return (
        jnp.sum(primal * primal, keepdims=True),
        penalty * penalty * jnp.sum(moved * moved, keepdims=True),
    )


def third_kernel(
    odd_ref, own_ref, inner_ref, outer_ref, gain_ref, start_ref, duals_ref, total, weight,
    sum_ref, gain_out, fresh_ref, duals_out, norms_ref,
):
    fresh = smoothed(odd_ref[0] == 1, own_ref[...], inner_ref[...], outer_ref[...])
    gain = gain_ref[...]
    duals = duals_ref[...] + gain - fresh
    first, second = gaps(gain, fresh, start_ref[...])
    gain = solved(total[...], weight[...], gain, fresh - duals)
    gain_out[...] = gain
    fresh_ref[...] = fresh
    duals_out[...] = duals
    sum_ref[...] = gain + duals
    lane = iota((1, LANES), 1)
    norms_ref[...] = jnp.where(lane == 0, first, jnp.where(lane == 1, second, 0.0))


def fourth_kernel(
    odd_ref, own_ref, inner_ref, outer_ref, gain_ref, fresh_ref, duals_ref, norms_ref,
    fresh_out, duals_out, norms_out,
):
    fresh = smoothed(odd_ref[0] == 1, own_ref[...], inner_ref[...], outer_ref[...])
    gain = gain_ref[...]
    duals = duals_ref[...] + gain - fresh
    first, second = gaps(gain, fresh, fresh_ref[...])
    lane = iota((1, LANES), 1)
    norms = norms_ref[...] + jnp.where(lane == 2, first, jnp.where(lane == 3, second, 0.0))
    norms_out[...] = jnp.broadcast_to(norms[None], norms_out.shape)
    rows_last(fresh, fresh_out)
    rows_last(duals, duals_out)


def turn_kernel(gain_ref, out_ref):
    rows_last(gain_ref[...], out_ref)


def call(kernel, outs, ins, scratch=(), smem=(), flops=0):
    return pl.pallas_call(
        kernel,
        out_shape=[jax.ShapeDtypeStruct(shape, F32) for shape in outs],
        in_specs=[
            pl.BlockSpec(memory_space=pltpu.SMEM if i in smem else pltpu.VMEM)
            for i in range(len(ins))
        ],
        out_specs=[pl.BlockSpec(memory_space=pltpu.VMEM) for _ in outs],
        scratch_shapes=scratch,
        cost_estimate=pl.CostEstimate(flops=flops, bytes_accessed=1000, transcendentals=0),
        compiler_params=pltpu.CompilerParams(vmem_limit_bytes=48 * 1024 * 1024),
        name=kernel.__name__,
    )(*ins)


def local(visibility, coherency, jones_start, duals_start):
    cards = lax.axis_size("chan")
    entries = jones_start.size * cards
    odd = (lax.axis_index("chan") % 2).astype(jnp.int32).reshape(1)
    inner = [(i, i ^ 1) for i in range(cards)]
    outer = [(i, i - 1 if i % 2 == 0 else i + 1) for i in range(cards)]
    outer = [(a, b) for a, b in outer if 0 <= b < cards]
    state = (M, 2 * LANES)
    work = [
        pltpu.VMEM((2, GROUP * 128, 256), BF16),
        pltpu.VMEM((2, GROUP * M, 256), F32),
        pltpu.VMEM((2, GROUP * 128, LANES), F32),
    ]
    sums, gain, start, duals, ct, vt = call(
        first_kernel,
        [state, state, state, state, (M * M, 256), (M * M, 256)],
        (
            coherency.reshape(2, 2, 16, 4, PAIRS),
            visibility.reshape(2, 2, 4, PAIRS),
            jones_start,
            duals_start,
        ),
        [
            pltpu.VMEM((256, 31 * LANES), BF16),
            pltpu.VMEM((48, 31 * LANES), BF16),
            pltpu.VMEM(state, F32),
            pltpu.VMEM((M, LANES), F32),
            *work,
        ],
        flops=10**10,
    )

    def swapped(x):
        return lax.ppermute(x, "chan", inner), lax.ppermute(x, "chan", outer)

    near, far = swapped(sums)
    total, weight = call(
        second_kernel, [state, (M, LANES)], (ct, vt, gain), work, flops=10**10
    )
    sums, gain, fresh, duals, norms = call(
        third_kernel,
        [state, state, state, state, (1, LANES)],
        (odd, sums, near, far, gain, start, duals, total, weight),
        smem=(0,),
    )
    near, far = swapped(sums)
    shape = jones_start.shape
    (jones_now,) = call(turn_kernel, [shape], (gain,), flops=10**9)
    consensus, duals_now, norms = call(
        fourth_kernel,
        [shape, shape, (cards, 1, LANES)],
        (odd, sums, near, far, gain, fresh, duals, norms),
        smem=(0,),
    )
    norms = lax.all_to_all(norms, "chan", split_axis=0, concat_axis=0, tiled=True)
    norms = jnp.sum(norms[:, 0, :4], axis=0).reshape(2, 2) / entries
    return jones_now, consensus, duals_now, norms


def solution(mesh):
    placed = (
        P(None, None, "chan", "slot", None),
        P(None, None, None, "chan", "slot", None),
        P(None, None, "slot", "chan", None),
        P(None, None, "slot", "chan", None),
    )
    return jax.shard_map(
        local,
        mesh=mesh,
        in_specs=placed,
        out_specs=(
            P(None, None, "slot", "chan", None),
            P(None, None, "slot", "chan", None),
            P(None, None, "slot", "chan", None),
            P("slot", None),
        ),
        check_vma=False,
    )
```

time: 161 us -> 55.6 us (0.35)
  local copies, waits for them, and re-layouts: 85.3 us -> 7.21 us
  other arithmetic: 34.8 us -> 0.09 us
  Pallas kernels: 0 us -> 15.6 us
  starting transfers between devices: 25.2 us -> 21.2 us
    mul x19 -> x0, local copies, waits for them, and re-layouts: 59.9 us -> none  [the longest x11 31.1 us: jones_update(): half_real = left_real * sky_real - left_imag * sky_imag]
    reduce_sum x6 -> x1, other arithmetic: 27.4 us -> 0.08 us  [local(): norms = jnp.sum(norms[:, 0, :4], axis=0).reshape(2, 2) / entries]
    convert_element_type x2 -> x0, local copies, waits for them, and re-layouts: 16.6 us -> none  [the longest x1 8.38 us: jones_update(): sky_real = coherency[0].astype(jnp.float32).reshape(grid_shape)]
    pallas_call x0 -> x5, Pallas kernels: none -> 15.6 us  [call(): pl.pallas_call(kernel, out_shape=[jax.ShapeDtypeStruct(shape, F32) for sh...]
    unnamed x17 -> x9, local copies, waits for them, and re-layouts: 2.15 us -> 6.57 us
    ppermute x4, starting transfers between devices: 12.4 us -> 9.03 us  [swapped(): return (lax.ppermute(x, 'chan', inner), lax.ppermute(x, 'chan', outer))]
    slice x2 -> x0, local copies, waits for them, and re-layouts: 3.14 us -> none  [the longest x1 2.38 us: jones_update(): sky_real = coherency[0].astype(jnp.float32).reshape(grid_shape)]
    ppermute x4, waiting for transfers between devices: 4.36 us -> 1.84 us  [swapped(): return (lax.ppermute(x, 'chan', inner), lax.ppermute(x, 'chan', outer))]
  transfers between devices with their start and end apart: 5 -> 5, of which waited for: 2 -> 2; matrix products, arithmetic and copies ran while one was open for 30% -> 0% of each run, Pallas kernels for 0% -> 11%
where the time goes in v1:
time: 55.6 us; the launch traced here: 55.3 us
  starting transfers between devices  21.2 us (38%)
  Pallas kernels  15.6 us (28%)
  waiting for transfers between devices  10.4 us (19%)
  local copies, waits for them, and re-layouts  7.21 us (13%)
  between operations  0.74 us (1%)
    pallas_call x5, Pallas kernels, call(): pl.pallas_call(kernel, out_shape=[jax.ShapeDtypeStruct(shape, F32) for sh...  15.6 us
    all_to_all x1, starting transfers between devices, local(): lax.all_to_all(norms, 'chan', split_axis=0, concat_axis=0, tiled=True)  12.2 us
    ppermute x4, starting transfers between devices, swapped(): return (lax.ppermute(x, 'chan', inner), lax.ppermute(x, 'chan', outer))  9.03 us
    all_to_all x1, waiting for transfers between devices, local(): lax.all_to_all(norms, 'chan', split_axis=0, concat_axis=0, tiled=True)  8.56 us
    unnamed x9, local copies, waits for them, and re-layouts  6.57 us
    ppermute x4, waiting for transfers between devices, swapped(): return (lax.ppermute(x, 'chan', inner), lax.ppermute(x, 'chan', outer))  1.84 us
  transfers between devices with their start and end apart: 5, of which 2 were waited for; matrix products, arithmetic and copies ran while one was open for 0% of the time, Pallas kernels for 11%

profile of v1, /device:TPU:1, one launch (start us, length us, event | category | flops | bytes accessed | tf_op | source)
XLA Modules:
  0.0 55.3 jit_solution(13336912523438599127)
XLA Ops:
  0.6 1.0 %copy.10 = f32[2,2,4,1,3844]{4,2,3,1,0:T(4,128)S(1)} copy(f32[2,2,4,1,3844]{4,3,2,1,0:T(1,128)} %param.4) | data formatting | bytes 492032
  1.6 0.0 copy-start
  1.7 1.6 %copy-done = bf16[2,2,16,4,1,3844]{5,3,4,2,1,0:T(4,128)(2,1)S(1)} copy-done((bf16[2,2,16,4,1,3844]{5,3,4,2,1,0:T(4,128)(2,1)S(1)}, bf16[2,2,16,4,1,3844]{5,3,4,2,1,0:T(4,128)(2,1)}, u32[]{:S(2)}) %copy-start) | copy-done | bytes 1968152
  3.2 0.0 copy-start.1
  3.2 0.9 %copy-done.1 = f32[2,2,16,4,62]{4,3,2,1,0:T(4,128)S(1)} copy-done((f32[2,2,16,4,62]{4,3,2,1,0:T(4,128)S(1)}, f32[2,2,16,4,62]{4,3,2,1,0:T(4,128)}, u32[]{:S(2)}) %copy-start.1) | copy-done | bytes 63512
  4.1 0.0 copy-start.2
  4.1 0.9 %copy-done.2 = f32[2,2,16,4,62]{4,3,2,1,0:T(4,128)S(1)} copy-done((f32[2,2,16,4,62]{4,3,2,1,0:T(4,128)S(1)}, f32[2,2,16,4,62]{4,3,2,1,0:T(4,128)}, u32[]{:S(2)}) %copy-start.2) | copy-done | bytes 63512
  5.0 7.5 %first_kernel.1 = (f32[64,256]{1,0:T(8,128)S(1)}, f32[64,256]{1,0:T(8,128)S(1)}, f32[64,256]{1,0:T(8,128)S(1)}, f32[64,256]{1,0:T(8,128)S(1)}, f32[4096,256]{1,0:T(8,128)}, /*index=5*/f32[4096,256]{1,0:T(8,128)}) custom-call(bf16[2,2,16,4,3844]{4,3,2,1,0:T(4,128)(2,1)S(1)} %bitcast.6, f32[2,2,4,3844]{3,2,1,0:T(4,128)S(1)} %bitcast.5, ...), custom_call_target="tpu_custom_call" | custom-call | flops 10000000000 | bytes 1000 | tf_op jit(solution)/shard_map/first_kernel/pallas_call | solution.py:236
  12.5 4.9 %collective-permute-start.1 = (f32[64,256]{1,0:T(8,128)S(1)}, f32[64,256]{1,0:T(8,128)S(1)}, u32[]{:S(2)}, u32[]{:S(2)}) collective-permute-start(f32[64,256]{1,0:T(8,128)S(1)} %get-tuple-element.20.own_ref), channel_id=1, source_target_pairs={{4,8},{8,4},{12,16},{16,12},{20,24},{24,20},{28,32},{32,28},{36,40... | collective-permute-start | bytes 196616 | tf_op jit(solution)/shard_map/ppermute | solution.py:284
  17.5 0.1 collective-permute-start
  17.6 0.0 copy-start.3
  17.6 2.2 %copy-done.3 = f32[4096,256]{1,0:T(8,128)S(1)} copy-done((f32[4096,256]{1,0:T(8,128)S(1)}, f32[4096,256]{1,0:T(8,128)}, u32[]{:S(2)}) %copy-start.3) | copy-done | bytes 4194328
  19.8 5.4 %second_kernel.1 = (f32[64,256]{1,0:T(8,128)S(1)}, f32[64,128]{1,0:T(8,128)S(1)}) custom-call(f32[4096,256]{1,0:T(8,128)S(1)} %copy-done.3, f32[4096,256]{1,0:T(8,128)} %get-tuple-element.25.vt, f32[64,256]{1,0:T(8,128)S(1)} %get-tuple-element.21.gain_ref), custom_call_target="tpu_custom_call" | custom-call | flops 10000000000 | bytes 1000 | tf_op jit(solution)/shard_map/second_kernel/pallas_call | solution.py:236
  25.1 0.0 collective-permute-done.1.outer_ref
  25.1 0.0 collective-permute-done.inner_ref
  25.2 0.6 %third_kernel.1 = (f32[64,256]{1,0:T(8,128)S(1)}, f32[64,256]{1,0:T(8,128)S(1)}, f32[64,256]{1,0:T(8,128)S(1)}, f32[64,256]{1,0:T(8,128)S(1)}, f32[1,128]{1,0:T(1,128)S(1)}) custom-call(s32[1]{0:T(128)} %bitcast.odd_ref, f32[64,256]{1,0:T(8,128)S(1)} %get-tuple-element.20.own_ref, f32[64,256]{1,0:T(8,128)S(1)} %collective-permute-done.inner_ref, ...), custom_call_target="tpu_custom_call" | custom-call | bytes 1000 | tf_op jit(solution)/shard_map/third_kernel/pallas_call | solution.py:236
  25.8 3.9 %collective-permute-start.3 = (f32[64,256]{1,0:T(8,128)S(1)}, f32[64,256]{1,0:T(8,128)S(1)}, u32[]{:S(2)}, u32[]{:S(2)}) collective-permute-start(f32[64,256]{1,0:T(8,128)S(1)} %get-tuple-element.29.own_ref), channel_id=1, source_target_pairs={{4,8},{8,4},{12,16},{16,12},{20,24},{24,20},{28,32},{32,28},{36,40... | collective-permute-start | bytes 196616 | tf_op jit(solution)/shard_map/ppermute | solution.py:284
  29.7 0.1 collective-permute-start.2
  29.8 1.8 %collective-permute-done.3.outer_ref = f32[64,256]{1,0:T(8,128)S(1)} collective-permute-done((f32[64,256]{1,0:T(8,128)S(1)}, f32[64,256]{1,0:T(8,128)S(1)}, u32[]{:S(2)}, u32[]{:S(2)}) %collective-permute-start.3) | collective-permute-done | bytes 65568 | tf_op jit(solution)/shard_map/ppermute | solution.py:284
  31.7 0.0 collective-permute-done.2.inner_ref
  31.7 1.4 %fourth_kernel.1 = (f32[2,2,16,4,62]{4,3,2,1,0:T(4,128)}, f32[2,2,16,4,62]{4,3,2,1,0:T(4,128)}, f32[64,1,128]{2,1,0:T(1,128)}) custom-call(s32[1]{0:T(128)} %bitcast.odd_ref, f32[64,256]{1,0:T(8,128)S(1)} %get-tuple-element.29.own_ref, f32[64,256]{1,0:T(8,128)S(1)} %collective-permute-done.2.inner_ref, f32[64,256]{1,0:T(8,128)S(1)} %collective-permute-done.3.outer_ref, ...), custom_call_target="tpu_custom_call" | custom-call | bytes 1000 | tf_op jit(solution)/shard_map/fourth_kernel/pallas_call | solution.py:236
  33.0 12.2 %all-to-all-start = ((f32[64,1,128]{2,1,0:T(1,128)}), f32[64,1,128]{2,1,0:T(1,128)S(1)}, u32[]{:S(2)}, u32[]{:S(2)}) async-start(f32[64,1,128]{2,1,0:T(1,128)} %get-tuple-element.35), calls=%async_computation | async-start | bytes 65536 | tf_op jit(solution)/shard_map/all_to_all | solution.py:305
  45.2 0.8 %turn_kernel.1 = f32[2,2,16,4,62]{4,3,2,1,0:T(4,128)} custom-call(f32[64,256]{1,0:T(8,128)S(1)} %get-tuple-element.28.gain_ref), custom_call_target="tpu_custom_call" | custom-call | flops 1000000000 | bytes 1000 | tf_op jit(solution)/shard_map/turn_kernel/pallas_call | solution.py:236
  46.0 8.6 %all-to-all-done = f32[64,1,128]{2,1,0:T(1,128)S(1)} async-done(((f32[64,1,128]{2,1,0:T(1,128)}), f32[64,1,128]{2,1,0:T(1,128)S(1)}, u32[]{:S(2)}, u32[]{:S(2)}) %all-to-all-start) | async-done | bytes 32800 | tf_op jit(solution)/shard_map/all_to_all | solution.py:305
  54.5 0.1 slice_reduce_fusion
  54.6 0.6 %div.6 = f32[2,2]{1,0:T(2,128)} reshape(f32[4]{0:T(128)S(1)} %broadcast_multiply_fusion) | data formatting | bytes 32 | tf_op jit(solution)/shard_map/div | solution.py:306
  (1 shorter events, 0.0 us)
Async XLA Ops:
  1.6 1.6 %copy-start = (bf16[2,2,16,4,1,3844]{5,3,4,2,1,0:T(4,128)(2,1)S(1)}, bf16[2,2,16,4,1,3844]{5,3,4,2,1,0:T(4,128)(2,1)}, u32[]{:S(2)}) copy-start(bf16[2,2,16,4,1,3844]{5,3,4,2,1,0:T(4,128)(2,1)} %param.5) | copy-start | bytes 5904388
  3.2 0.9 %copy-start.1 = (f32[2,2,16,4,62]{4,3,2,1,0:T(4,128)S(1)}, f32[2,2,16,4,62]{4,3,2,1,0:T(4,128)}, u32[]{:S(2)}) copy-start(f32[2,2,16,4,62]{4,3,2,1,0:T(4,128)} %jones_ref.1) | copy-start | bytes 190468
  4.1 0.9 %copy-start.2 = (f32[2,2,16,4,62]{4,3,2,1,0:T(4,128)S(1)}, f32[2,2,16,4,62]{4,3,2,1,0:T(4,128)}, u32[]{:S(2)}) copy-start(f32[2,2,16,4,62]{4,3,2,1,0:T(4,128)} %duals_ref.1) | copy-start | bytes 190468
  12.5 12.6 %collective-permute-start.1 = (f32[64,256]{1,0:T(8,128)S(1)}, f32[64,256]{1,0:T(8,128)S(1)}, u32[]{:S(2)}, u32[]{:S(2)}) collective-permute-start(f32[64,256]{1,0:T(8,128)S(1)} %get-tuple-element.20.own_ref), channel_id=1, source_target_pairs={{4,8},{8,4},{12,16},{16,12},{20,24},{24,20},{28,32},{32,28},{36,40... | collective-permute-start | bytes 196616 | tf_op jit(solution)/shard_map/ppermute | solution.py:284
  17.5 7.7 %collective-permute-start = (f32[64,256]{1,0:T(8,128)S(1)}, f32[64,256]{1,0:T(8,128)S(1)}, u32[]{:S(2)}, u32[]{:S(2)}) collective-permute-start(f32[64,256]{1,0:T(8,128)S(1)} %get-tuple-element.20.own_ref), channel_id=1, source_target_pairs={{0,4},{4,0},{8,12},{12,8},{16,20},{20,16},{24,28},{28,24},{32,36},... | collective-permute-start | bytes 196616 | tf_op jit(solution)/shard_map/ppermute | solution.py:284
  17.6 2.2 %copy-start.3 = (f32[4096,256]{1,0:T(8,128)S(1)}, f32[4096,256]{1,0:T(8,128)}, u32[]{:S(2)}) copy-start(f32[4096,256]{1,0:T(8,128)} %get-tuple-element.24.ct) | copy-start | bytes 12582916
  25.8 5.9 %collective-permute-start.3 = (f32[64,256]{1,0:T(8,128)S(1)}, f32[64,256]{1,0:T(8,128)S(1)}, u32[]{:S(2)}, u32[]{:S(2)}) collective-permute-start(f32[64,256]{1,0:T(8,128)S(1)} %get-tuple-element.29.own_ref), channel_id=1, source_target_pairs={{4,8},{8,4},{12,16},{16,12},{20,24},{24,20},{28,32},{32,28},{36,40... | collective-permute-start | bytes 196616 | tf_op jit(solution)/shard_map/ppermute | solution.py:284
  29.7 1.9 %collective-permute-start.2 = (f32[64,256]{1,0:T(8,128)S(1)}, f32[64,256]{1,0:T(8,128)S(1)}, u32[]{:S(2)}, u32[]{:S(2)}) collective-permute-start(f32[64,256]{1,0:T(8,128)S(1)} %get-tuple-element.29.own_ref), channel_id=1, source_target_pairs={{0,4},{4,0},{8,12},{12,8},{16,20},{20,16},{24,28},{28,24},{32,36},... | collective-permute-start | bytes 196616 | tf_op jit(solution)/shard_map/ppermute | solution.py:284
  33.0 21.5 %all-to-all-start = ((f32[64,1,128]{2,1,0:T(1,128)}), f32[64,1,128]{2,1,0:T(1,128)S(1)}, u32[]{:S(2)}, u32[]{:S(2)}) async-start(f32[64,1,128]{2,1,0:T(1,128)} %get-tuple-element.35), calls=%async_computation | async-start | bytes 65536 | tf_op jit(solution)/shard_map/all_to_all | solution.py:305

commit v2 on v1

--- a/solution.py
+++ b/solution.py
@@ -13,6 +13,7 @@
 PAIRS = N * N
 F32 = jnp.float32
 BF16 = jnp.bfloat16
+ROWS = 31 * LANES
 GROUP = 4
 
 
@@ -39,27 +40,24 @@
                 ref[part, pol, k] = half[at : at + 4, :N]
 
 
-def lay_out(coh_ref, vis_ref, flat, vflat, ct, vt):
-    width = 31 * LANES
-    flat[:, width - LANES :] = jnp.zeros((256, LANES), BF16)
-    vflat[:, width - LANES :] = jnp.zeros((48, LANES), BF16)
-    for part in range(2):
-        for pol in range(2):
-            for k in range(0, 16, 4):
-                at = part * 128 + pol * 64 + k * 4
-                block = [coh_ref[part, pol, k + i].astype(F32) for i in range(4)]
-                flat[at : at + 16, :PAIRS] = jnp.concatenate(block, axis=0).astype(BF16)
-    v = jnp.concatenate([vis_ref[part, pol] for part in range(2) for pol in range(2)], axis=0)
+def lay_out(coh_ref, vis_ref, vflat, short, ct, vt, copies):
+    vflat[:, ROWS - LANES :] = jnp.zeros((48, LANES), BF16)
+    copies[0].wait()
+    v = jnp.concatenate(
+        [vis_ref[a, b, f] for a in range(2) for b in range(2) for f in range(4)], axis=0
+    )
     for split in range(3):
         high = v.astype(BF16)
         vflat[split * 16 : split * 16 + 16, :PAIRS] = high
         v = v - high.astype(F32)
-    row = iota((128, 256), 0)
-    col = iota((128, 256), 1)
-    half = row // M
-    q = row % M
-    lag = jnp.where(q < N, col - half * N - q, 1000)
-    own = q - half
+    same = jnp.where(iota((LANES, LANES), 0) == iota((LANES, LANES), 1), 1.0, 0.0).astype(BF16)
+    for start in range(0, ROWS, LANES):
+        short[start : start + LANES] = lax.dot_general(
+            same,
+            vflat[:, start : start + LANES],
+            (((1,), (1,)), ((), ())),
+            preferred_element_type=F32,
+        ).astype(BF16)
     source = iota((48, 256), 0)
     target = iota((48, 256), 1)
     spread = (
@@ -68,22 +66,29 @@
         & (source % 4 == target % 4)
     )
     spread = jnp.where(spread, 1.0, 0.0).astype(BF16)
-    for t in range(31):
-        start = 124 * t // LANES * LANES
-        shift = 124 * t - start
-        pick = jnp.where((lag == shift) & (own != 2 * t), 1.0, 0.0).astype(BF16)
-        contract = (((1,), (1,)), ((), ()))
-        ct[t * 128 : t * 128 + 128] = lax.dot_general(
-            pick, flat[:, start : start + 256], contract, preferred_element_type=F32
+    for start in range(0, ROWS, ROWS // 4):
+        wide = jnp.dot(
+            short[start : start + ROWS // 4], spread, preferred_element_type=F32
         )
-        short = lax.dot_general(
-            pick, vflat[:, start : start + 256], contract, preferred_element_type=F32
-        )
-        vt[t * 128 : t * 128 + 128] = jnp.dot(
-            short.astype(BF16), spread, preferred_element_type=F32
-        )
-    ct[31 * 128 :] = jnp.zeros((128, 256), F32)
-    vt[31 * 128 :] = jnp.zeros((128, 256), F32)
+        vt[0, start : start + ROWS // 4] = wide[:, :LANES]
+        vt[1, start : start + ROWS // 4] = wide[:, LANES:]
+    for part in range(2):
+        copies[1 + part * 2].wait()
+        copies[2 + part * 2].wait()
+        for start in range(0, ROWS, LANES):
+            x = jnp.concatenate(
+                [
+                    coh_ref[part, pol, k, :, start : min(start + LANES, PAIRS)].astype(F32)
+                    for pol in range(2)
+                    for k in range(16)
+                ],
+                axis=0,
+            )
+            if x.shape[1] < LANES:
+                x = jnp.concatenate([x, jnp.zeros((LANES, LANES - x.shape[1]), F32)], axis=1)
+            ct[part, start : start + LANES] = x.T
+        for p in range(N):
+            ct[part, p * N + p : p * N + p + 1] = jnp.zeros((1, LANES), F32)
 
 
 def pair_sums(ct, vt, gain, total, weight, lhs, half, model):
@@ -92,12 +97,15 @@
     same = (row // 64 == col // 64) & (row % 4 == col % 4)
     adder = jnp.where(same, 1.0, 0.0).astype(BF16)
 
+    def count(group):
+        return min(GROUP, N - group * GROUP)
+
     def front(group):
         slot = group % 2
-        for i in range(GROUP):
+        for i in range(count(group)):
             p = group * GROUP + i
-            c_real = ct[p * M : p * M + M, :LANES]
-            c_imag = ct[p * M : p * M + M, LANES:]
+            c_real = ct[0, p * N : p * N + M]
+            c_imag = ct[1, p * N : p * N + M]
             q_real = gain[:, :LANES]
             q_imag = gain[:, LANES:]
             h_real = c_real * q_real + c_imag * q_imag
@@ -113,16 +121,17 @@
                 high = m.astype(BF16)
                 lhs[slot, at : at + M, :LANES] = high
                 lhs[slot, at : at + M, LANES:] = (m - high.astype(F32)).astype(BF16)
-        model[slot] = jnp.dot(lhs[slot], adder, preferred_element_type=F32)
+        rows = count(group) * 128
+        model[slot, :rows] = jnp.dot(lhs[slot, :rows], adder, preferred_element_type=F32)
 
     def back(group):
         slot = group % 2
-        for i in range(GROUP):
+        for i in range(count(group)):
             p = group * GROUP + i
             h_real = half[slot, i * M : i * M + M, :LANES]
             h_imag = half[slot, i * M : i * M + M, LANES:]
-            d_real = vt[p * M : p * M + M, :LANES] - model[slot, i * 128 : i * 128 + M]
-            d_imag = vt[p * M : p * M + M, LANES:] - model[slot, i * 128 + M : i * 128 + 128]
+            d_real = vt[0, p * N : p * N + M] - model[slot, i * 128 : i * 128 + M]
+            d_imag = vt[1, p * N : p * N + M] - model[slot, i * 128 + M : i * 128 + 128]
 
             def over_q(x):
                 return jnp.sum(x, axis=0, keepdims=True)
@@ -131,6 +140,8 @@
             total[p : p + 1, LANES:] = over_q(d_imag * h_real - d_real * h_imag)
             weight[p : p + 1] = over_q(h_real * h_real + h_imag * h_imag)
 
+    total[N:] = jnp.zeros((M - N, 2 * LANES), F32)
+    weight[N:] = jnp.zeros((M - N, LANES), F32)
     front(0)
     for group in range(M // GROUP):
         if group + 1 < M // GROUP:
@@ -144,13 +155,28 @@
 
 
 def first_kernel(
-    coh_ref, vis_ref, jones_ref, duals_ref,
+    coh_hbm, vis_hbm, jones_hbm, duals_hbm,
     sum_ref, gain_ref, start_ref, duals_out, ct, vt,
-    flat, vflat, total, weight, lhs, half, model,
+    coh_ref, vis_ref, jones_ref, duals_ref, vflat, short, total, weight, lhs, half, model, arrived,
 ):
-    lay_out(coh_ref, vis_ref, flat, vflat, ct, vt)
+    copies = [
+        pltpu.make_async_copy(source, target, arrived.at[i])
+        for i, (source, target) in enumerate(
+            [
+                (jones_hbm, jones_ref),
+                (duals_hbm, duals_ref),
+                (vis_hbm, vis_ref),
+                *((coh_hbm.at[a, b], coh_ref.at[a, b]) for a in range(2) for b in range(2)),
+            ]
+        )
+    ]
+    for copy in copies:
+        copy.start()
+    copies[0].wait()
     start_ref[...] = rows_first(jones_ref)
+    copies[1].wait()
     duals_out[...] = rows_first(duals_ref)
+    lay_out(coh_ref, vis_ref, vflat, short, ct, vt, copies[2:])
     pair_sums(ct, vt, start_ref, total, weight, lhs, half, model)
     gain = solved(total[...], weight[...], start_ref[...], start_ref[...] - duals_out[...])
     gain_ref[...] = gain
@@ -224,26 +250,27 @@
     lane = iota((1, LANES), 1)
     norms = norms_ref[...] + jnp.where(lane == 2, first, jnp.where(lane == 3, second, 0.0))
     norms_out[...] = jnp.broadcast_to(norms[None], norms_out.shape)
-    rows_last(fresh, fresh_out)
-    rows_last(duals, duals_out)
-
-
-def turn_kernel(gain_ref, out_ref):
-    rows_last(gain_ref[...], out_ref)
-
-
-def call(kernel, outs, ins, scratch=(), smem=(), flops=0):
+    fresh_out[...] = fresh
+    duals_out[...] = duals
+
+
+def turn_kernel(*refs):
+    for source, target in zip(refs[: len(refs) // 2], refs[len(refs) // 2 :]):
+        rows_last(source[...], target)
+
+
+def call(kernel, outs, ins, scratch=(), smem=(), hbm=(), flops=0):
+    def space(i):
+        return pltpu.SMEM if i in smem else pltpu.HBM if i in hbm else pltpu.VMEM
+
     return pl.pallas_call(
         kernel,
         out_shape=[jax.ShapeDtypeStruct(shape, F32) for shape in outs],
-        in_specs=[
-            pl.BlockSpec(memory_space=pltpu.SMEM if i in smem else pltpu.VMEM)
-            for i in range(len(ins))
-        ],
+        in_specs=[pl.BlockSpec(memory_space=space(i)) for i in range(len(ins))],
         out_specs=[pl.BlockSpec(memory_space=pltpu.VMEM) for _ in outs],
         scratch_shapes=scratch,
         cost_estimate=pl.CostEstimate(flops=flops, bytes_accessed=1000, transcendentals=0),
-        compiler_params=pltpu.CompilerParams(vmem_limit_bytes=48 * 1024 * 1024),
+        compiler_params=pltpu.CompilerParams(vmem_limit_bytes=24 * 1024 * 1024),
         name=kernel.__name__,
     )(*ins)
 
@@ -263,20 +290,28 @@
     ]
     sums, gain, start, duals, ct, vt = call(
         first_kernel,
-        [state, state, state, state, (M * M, 256), (M * M, 256)],
+        [state, state, state, state, (2, ROWS, LANES), (2, ROWS, LANES)],
         (
-            coherency.reshape(2, 2, 16, 4, PAIRS),
-            visibility.reshape(2, 2, 4, PAIRS),
-            jones_start,
-            duals_start,
+            *(
+                pltpu.with_memory_space_constraint(x, pltpu.HBM)
+                for x in (
+                    coherency.reshape(2, 2, 16, 4, PAIRS), visibility, jones_start, duals_start
+                )
+            ),
         ),
         [
-            pltpu.VMEM((256, 31 * LANES), BF16),
-            pltpu.VMEM((48, 31 * LANES), BF16),
+            pltpu.VMEM((2, 2, 16, 4, PAIRS), BF16),
+            pltpu.VMEM(visibility.shape, F32),
+            pltpu.VMEM(jones_start.shape, F32),
+            pltpu.VMEM(duals_start.shape, F32),
+            pltpu.VMEM((48, ROWS), BF16),
+            pltpu.VMEM((ROWS, 48), BF16),
             pltpu.VMEM(state, F32),
             pltpu.VMEM((M, LANES), F32),
             *work,
+            pltpu.SemaphoreType.DMA((7,)),
         ],
+        hbm=(0, 1, 2, 3),
         flops=10**10,
     )
 
@@ -296,12 +331,13 @@
     near, far = swapped(sums)
     shape = jones_start.shape
     (jones_now,) = call(turn_kernel, [shape], (gain,), flops=10**9)
-    consensus, duals_now, norms = call(
+    fresh, duals, norms = call(
         fourth_kernel,
-        [shape, shape, (cards, 1, LANES)],
+        [state, state, (cards, 1, LANES)],
         (odd, sums, near, far, gain, fresh, duals, norms),
         smem=(0,),
     )
+    consensus, duals_now = call(turn_kernel, [shape, shape], (fresh, duals), flops=10**9)
     norms = lax.all_to_all(norms, "chan", split_axis=0, concat_axis=0, tiled=True)
     norms = jnp.sum(norms[:, 0, :4], axis=0).reshape(2, 2) / entries
     return jones_now, consensus, duals_now, norms

time: 55.6 us -> 46.1 us (0.83)
  local copies, waits for them, and re-layouts: 7.21 us -> 0.65 us
  Pallas kernels: 15.6 us -> 12.3 us
    unnamed x9 -> x0, local copies, waits for them, and re-layouts: 6.57 us -> none
    pallas_call x5 -> x6, Pallas kernels: 15.6 us -> 12.3 us  [call(): pl.pallas_call(kernel, out_shape=[jax.ShapeDtypeStruct(shape, F32) for sh...]
    all_to_all x1, starting transfers between devices: 12.2 us -> 12.9 us  [local(): lax.all_to_all(norms, 'chan', split_axis=0, concat_axis=0, tiled=True)]
  transfers between devices with their start and end apart: 5 -> 5, of which waited for: 2 -> 3; matrix products, arithmetic and copies ran while one was open for 0% -> 0% of each run, Pallas kernels for 11% -> 10%
where the time goes in v2:
time: 46.1 us; the launch traced here: 45.9 us
  starting transfers between devices  21.5 us (47%)
  Pallas kernels  12.3 us (27%)
  waiting for transfers between devices  10.6 us (23%)
  between operations  0.71 us (2%)
  local copies, waits for them, and re-layouts  0.65 us (1%)
    all_to_all x1, starting transfers between devices, local(): lax.all_to_all(norms, 'chan', split_axis=0, concat_axis=0, tiled=True)  12.9 us
    pallas_call x6, Pallas kernels, call(): pl.pallas_call(kernel, out_shape=[jax.ShapeDtypeStruct(shape, F32) for sh...  12.3 us
    all_to_all x1, waiting for transfers between devices, local(): lax.all_to_all(norms, 'chan', split_axis=0, concat_axis=0, tiled=True)  8.51 us
    ppermute x4, starting transfers between devices, swapped(): return (lax.ppermute(x, 'chan', inner), lax.ppermute(x, 'chan', outer))  8.51 us
    ppermute x4, waiting for transfers between devices, swapped(): return (lax.ppermute(x, 'chan', inner), lax.ppermute(x, 'chan', outer))  2.13 us
  transfers between devices with their start and end apart: 5, of which 3 were waited for; matrix products, arithmetic and copies ran while one was open for 0% of the time, Pallas kernels for 10%

profile of v2, /device:TPU:1, one launch (start us, length us, event | category | flops | bytes accessed | tf_op | source)
XLA Modules:
  0.0 45.9 jit_solution(8566650610238704512)
XLA Ops:
  0.6 5.8 %first_kernel.1 = (f32[64,256]{1,0:T(8,128)S(1)}, f32[64,256]{1,0:T(8,128)S(1)}, f32[64,256]{1,0:T(8,128)S(1)}, f32[64,256]{1,0:T(8,128)S(1)}, f32[2,3968,128]{2,1,0:T(8,128)S(1)}, /*index=5*/f32[2,3968,128]{2,1,0:T(8,128)S(1)}) custom-call(bf16[2,2,16,4,3844]{4,3,2,1,0:T(4,128)(2,1)} %bitcast.2, f32[2,2,4,1,3844]{4,3,2,1,0:T(1,128)} %vis_hbm.1, ...), custom_call_target="tpu_custom_call" | custom-call | flops 10000000000 | bytes 1000 | tf_op jit(solution)/shard_map/first_kernel/pallas_call | solution.py:266
  6.4 3.3 %collective-permute-start = (f32[64,256]{1,0:T(8,128)S(1)}, f32[64,256]{1,0:T(8,128)S(1)}, u32[]{:S(2)}, u32[]{:S(2)}) collective-permute-start(f32[64,256]{1,0:T(8,128)S(1)} %get-tuple-element.22.own_ref), channel_id=1, source_target_pairs={{0,4},{4,0},{8,12},{12,8},{16,20},{20,16},{24,28},{28,24},{32,36},... | collective-permute-start | bytes 196616 | tf_op jit(solution)/shard_map/ppermute | solution.py:319
  9.7 1.9 %collective-permute-start.1 = (f32[64,256]{1,0:T(8,128)S(1)}, f32[64,256]{1,0:T(8,128)S(1)}, u32[]{:S(2)}, u32[]{:S(2)}) collective-permute-start(f32[64,256]{1,0:T(8,128)S(1)} %get-tuple-element.22.own_ref), channel_id=1, source_target_pairs={{4,8},{8,4},{12,16},{16,12},{20,24},{24,20},{28,32},{32,28},{36,40... | collective-permute-start | bytes 196616 | tf_op jit(solution)/shard_map/ppermute | solution.py:319
  11.6 3.1 %second_kernel.1 = (f32[64,256]{1,0:T(8,128)S(1)}, f32[64,128]{1,0:T(8,128)S(1)}) custom-call(f32[2,3968,128]{2,1,0:T(8,128)S(1)} %get-tuple-element.26.ct, f32[2,3968,128]{2,1,0:T(8,128)S(1)} %get-tuple-element.27.vt, f32[64,256]{1,0:T(8,128)S(1)} %get-tuple-element.23.gain_ref), custom_call_target="tpu_custom_call" | custom-call | flops 10000000000 | bytes 1000 | tf_op jit(solution)/shard_map/second_kernel/pallas_call | solution.py:266
  14.7 0.0 collective-permute-done.inner_ref
  14.7 0.5 %collective-permute-done.1.outer_ref = f32[64,256]{1,0:T(8,128)S(1)} collective-permute-done((f32[64,256]{1,0:T(8,128)S(1)}, f32[64,256]{1,0:T(8,128)S(1)}, u32[]{:S(2)}, u32[]{:S(2)}) %collective-permute-start.1) | collective-permute-done | bytes 65568 | tf_op jit(solution)/shard_map/ppermute | solution.py:319
  15.3 0.6 %third_kernel.1 = (f32[64,256]{1,0:T(8,128)S(1)}, f32[64,256]{1,0:T(8,128)S(1)}, f32[64,256]{1,0:T(8,128)S(1)}, f32[64,256]{1,0:T(8,128)S(1)}, f32[1,128]{1,0:T(1,128)S(1)}) custom-call(s32[1]{0:T(128)} %bitcast.odd_ref, f32[64,256]{1,0:T(8,128)S(1)} %get-tuple-element.22.own_ref, f32[64,256]{1,0:T(8,128)S(1)} %collective-permute-done.inner_ref, ...), custom_call_target="tpu_custom_call" | custom-call | bytes 1000 | tf_op jit(solution)/shard_map/third_kernel/pallas_call | solution.py:266
  15.9 0.1 collective-permute-start.2
  16.0 3.2 %collective-permute-start.3 = (f32[64,256]{1,0:T(8,128)S(1)}, f32[64,256]{1,0:T(8,128)S(1)}, u32[]{:S(2)}, u32[]{:S(2)}) collective-permute-start(f32[64,256]{1,0:T(8,128)S(1)} %get-tuple-element.31.own_ref), channel_id=1, source_target_pairs={{4,8},{8,4},{12,16},{16,12},{20,24},{24,20},{28,32},{32,28},{36,40... | collective-permute-start | bytes 196616 | tf_op jit(solution)/shard_map/ppermute | solution.py:319
  19.3 0.8 %turn_kernel.2 = f32[2,2,16,4,62]{4,3,2,1,0:T(4,128)} custom-call(f32[64,256]{1,0:T(8,128)S(1)} %get-tuple-element.30.refs_0_.gain_ref), custom_call_target="tpu_custom_call" | custom-call | flops 1000000000 | bytes 1000 | tf_op jit(solution)/shard_map/turn_kernel/pallas_call | solution.py:266
  20.0 0.0 collective-permute-done.2.inner_ref
  20.0 1.6 %collective-permute-done.3.outer_ref = f32[64,256]{1,0:T(8,128)S(1)} collective-permute-done((f32[64,256]{1,0:T(8,128)S(1)}, f32[64,256]{1,0:T(8,128)S(1)}, u32[]{:S(2)}, u32[]{:S(2)}) %collective-permute-start.3) | collective-permute-done | bytes 65568 | tf_op jit(solution)/shard_map/ppermute | solution.py:319
  21.6 1.3 %fourth_kernel.1 = (f32[64,256]{1,0:T(8,128)S(1)}, f32[64,256]{1,0:T(8,128)S(1)}, f32[64,1,128]{2,1,0:T(1,128)}) custom-call(s32[1]{0:T(128)} %bitcast.odd_ref, f32[64,256]{1,0:T(8,128)S(1)} %get-tuple-element.31.own_ref, f32[64,256]{1,0:T(8,128)S(1)} %collective-permute-done.2.inner_ref, f32[64,256]{1,0:T(8,128)S(1)} %collective-permute-done.3.outer_ref, ...), custom_call_target="tpu_custom_call" | custom-call | bytes 1000 | tf_op jit(solution)/shard_map/fourth_kernel/pallas_call | solution.py:266
  22.9 12.9 %all-to-all-start = ((f32[64,1,128]{2,1,0:T(1,128)}), f32[64,1,128]{2,1,0:T(1,128)S(1)}, u32[]{:S(2)}, u32[]{:S(2)}) async-start(f32[64,1,128]{2,1,0:T(1,128)} %get-tuple-element.39), calls=%async_computation | async-start | bytes 65536 | tf_op jit(solution)/shard_map/all_to_all | solution.py:341
  35.8 0.8 %turn_kernel.3 = (f32[2,2,16,4,62]{4,3,2,1,0:T(4,128)}, f32[2,2,16,4,62]{4,3,2,1,0:T(4,128)}) custom-call(f32[64,256]{1,0:T(8,128)S(1)} %get-tuple-element.35.refs_0_, f32[64,256]{1,0:T(8,128)S(1)} %get-tuple-element.36.refs_1_), custom_call_target="tpu_custom_call" | custom-call | flops 1000000000 | bytes 1000 | tf_op jit(solution)/shard_map/turn_kernel/pallas_call | solution.py:266
  36.6 8.5 %all-to-all-done = f32[64,1,128]{2,1,0:T(1,128)S(1)} async-done(((f32[64,1,128]{2,1,0:T(1,128)}), f32[64,1,128]{2,1,0:T(1,128)S(1)}, u32[]{:S(2)}, u32[]{:S(2)}) %all-to-all-start) | async-done | bytes 32800 | tf_op jit(solution)/shard_map/all_to_all | solution.py:341
  45.1 0.1 slice_reduce_fusion
  45.2 0.6 %div.6 = f32[2,2]{1,0:T(2,128)} reshape(f32[4]{0:T(128)S(1)} %broadcast_multiply_fusion) | data formatting | bytes 32 | tf_op jit(solution)/shard_map/div | solution.py:342
  (1 shorter events, 0.0 us)
Async XLA Ops:
  6.4 8.3 %collective-permute-start = (f32[64,256]{1,0:T(8,128)S(1)}, f32[64,256]{1,0:T(8,128)S(1)}, u32[]{:S(2)}, u32[]{:S(2)}) collective-permute-start(f32[64,256]{1,0:T(8,128)S(1)} %get-tuple-element.22.own_ref), channel_id=1, source_target_pairs={{0,4},{4,0},{8,12},{12,8},{16,20},{20,16},{24,28},{28,24},{32,36},... | collective-permute-start | bytes 196616 | tf_op jit(solution)/shard_map/ppermute | solution.py:319
  9.7 5.6 %collective-permute-start.1 = (f32[64,256]{1,0:T(8,128)S(1)}, f32[64,256]{1,0:T(8,128)S(1)}, u32[]{:S(2)}, u32[]{:S(2)}) collective-permute-start(f32[64,256]{1,0:T(8,128)S(1)} %get-tuple-element.22.own_ref), channel_id=1, source_target_pairs={{4,8},{8,4},{12,16},{16,12},{20,24},{24,20},{28,32},{32,28},{36,40... | collective-permute-start | bytes 196616 | tf_op jit(solution)/shard_map/ppermute | solution.py:319
  15.9 4.1 %collective-permute-start.2 = (f32[64,256]{1,0:T(8,128)S(1)}, f32[64,256]{1,0:T(8,128)S(1)}, u32[]{:S(2)}, u32[]{:S(2)}) collective-permute-start(f32[64,256]{1,0:T(8,128)S(1)} %get-tuple-element.31.own_ref), channel_id=1, source_target_pairs={{0,4},{4,0},{8,12},{12,8},{16,20},{20,16},{24,28},{28,24},{32,36},... | collective-permute-start | bytes 196616 | tf_op jit(solution)/shard_map/ppermute | solution.py:319
  16.0 5.6 %collective-permute-start.3 = (f32[64,256]{1,0:T(8,128)S(1)}, f32[64,256]{1,0:T(8,128)S(1)}, u32[]{:S(2)}, u32[]{:S(2)}) collective-permute-start(f32[64,256]{1,0:T(8,128)S(1)} %get-tuple-element.31.own_ref), channel_id=1, source_target_pairs={{4,8},{8,4},{12,16},{16,12},{20,24},{24,20},{28,32},{32,28},{36,40... | collective-permute-start | bytes 196616 | tf_op jit(solution)/shard_map/ppermute | solution.py:319
  22.9 22.3 %all-to-all-start = ((f32[64,1,128]{2,1,0:T(1,128)}), f32[64,1,128]{2,1,0:T(1,128)S(1)}, u32[]{:S(2)}, u32[]{:S(2)}) async-start(f32[64,1,128]{2,1,0:T(1,128)} %get-tuple-element.39), calls=%async_computation | async-start | bytes 65536 | tf_op jit(solution)/shard_map/all_to_all | solution.py:341

commit v3 on v2

--- a/solution.py
+++ b/solution.py
@@ -4,6 +4,7 @@
 from jax.experimental import pallas as pl
 from jax.experimental.pallas import tpu as pltpu
 from jax.sharding import PartitionSpec as P
+
 
 penalty = 8.0
 kernel_taps = (0.04, 0.06, 0.1, 0.15, 0.3, 0.15, 0.1, 0.06, 0.04)
@@ -154,9 +155,32 @@
     return (total + gain * twice + penalty * target) / (twice + penalty)
 
 
+def write_taps(card_ref, out_ref):
+    card = card_ref[0]
+    odd = lax.rem(card, 2) == 1
+    source = iota((LANES, LANES), 0)
+    target = iota((LANES, LANES), 1)
+    lag = jnp.where(source // 4 == target // 4, source % 4 - target % 4, 100)
+
+    def taps(shift):
+        out = jnp.zeros((LANES, LANES), F32)
+        for offset in range(-4, 5):
+            out = jnp.where(lag + shift == offset, kernel_taps[offset + 4], out)
+        return out
+
+    after, before = taps(4), taps(-4)
+    for i, weights in enumerate(
+        (taps(0), jnp.where(odd, before, after), jnp.where(odd, after, before))
+    ):
+        high = weights.astype(BF16)
+        low = (weights - high.astype(F32)).astype(BF16)
+        out_ref[i * LANES : i * LANES + LANES] = high
+        out_ref[(3 + i) * LANES : (4 + i) * LANES] = low
+
+
 def first_kernel(
-    coh_hbm, vis_hbm, jones_hbm, duals_hbm,
-    sum_ref, gain_ref, start_ref, duals_out, ct, vt,
+    coh_hbm, vis_hbm, jones_hbm, duals_hbm, card_ref,
+    sum_ref, gain_ref, start_ref, duals_out, taps_ref, ct, vt,
     coh_ref, vis_ref, jones_ref, duals_ref, vflat, short, total, weight, lhs, half, model, arrived,
 ):
     copies = [
@@ -172,6 +196,7 @@
     ]
     for copy in copies:
         copy.start()
+    write_taps(card_ref, taps_ref)
     copies[0].wait()
     start_ref[...] = rows_first(jones_ref)
     copies[1].wait()
@@ -187,30 +212,23 @@
     pair_sums(ct, vt, gain_ref, total, weight, lhs, half, model)
 
 
-def smoothed(odd, own, inner, outer):
-    source = iota((LANES, LANES), 0)
-    target = iota((LANES, LANES), 1)
-    lag = jnp.where(source // 4 == target // 4, source % 4 - target % 4, 100)
-
-    def taps(shift):
-        out = jnp.zeros((LANES, LANES), F32)
-        for offset in range(-4, 5):
-            out = jnp.where(lag + shift == offset, kernel_taps[offset + 4], out)
-        return out
-
-    after, before = taps(4), taps(-4)
-    weights = jnp.concatenate(
-        [taps(0), jnp.where(odd, before, after), jnp.where(odd, after, before)], axis=0
-    )
-    halves = []
-    for part in range(2):
-        x = jnp.concatenate(
-            [a[:, part * LANES : (part + 1) * LANES] for a in (own, inner, outer)], axis=1
-        )
-        halves.append(
-            jnp.dot(x, weights, precision=lax.Precision.HIGHEST, preferred_element_type=F32)
-        )
-    return jnp.concatenate(halves, axis=1)
+def smoothed(taps_ref, own, inner, outer):
+    x = jnp.concatenate(
+        [
+            jnp.concatenate([a[:, :LANES] for a in (own, inner, outer)], axis=1),
+            jnp.concatenate([a[:, LANES:] for a in (own, inner, outer)], axis=1),
+        ],
+        axis=0,
+    )
+    high = x.astype(BF16)
+    low = (x - high.astype(F32)).astype(BF16)
+
+    def dot(a, b):
+        return jnp.dot(a, b, preferred_element_type=F32)
+
+    top, rest = taps_ref[: 3 * LANES], taps_ref[3 * LANES :]
+    out = dot(high, top) + dot(low, top) + dot(high, rest)
+    return jnp.concatenate([out[:M], out[M:]], axis=1)
 
 
 def gaps(gain, fresh, consensus):
@@ -223,10 +241,10 @@
 
 
 def third_kernel(
-    odd_ref, own_ref, inner_ref, outer_ref, gain_ref, start_ref, duals_ref, total, weight,
+    taps_ref, own_ref, inner_ref, outer_ref, gain_ref, start_ref, duals_ref, total, weight,
     sum_ref, gain_out, fresh_ref, duals_out, norms_ref,
 ):
-    fresh = smoothed(odd_ref[0] == 1, own_ref[...], inner_ref[...], outer_ref[...])
+    fresh = smoothed(taps_ref, own_ref[...], inner_ref[...], outer_ref[...])
     gain = gain_ref[...]
     duals = duals_ref[...] + gain - fresh
     first, second = gaps(gain, fresh, start_ref[...])
@@ -240,10 +258,10 @@
 
 
 def fourth_kernel(
-    odd_ref, own_ref, inner_ref, outer_ref, gain_ref, fresh_ref, duals_ref, norms_ref,
+    taps_ref, own_ref, inner_ref, outer_ref, gain_ref, fresh_ref, duals_ref, norms_ref,
     fresh_out, duals_out, norms_out,
 ):
-    fresh = smoothed(odd_ref[0] == 1, own_ref[...], inner_ref[...], outer_ref[...])
+    fresh = smoothed(taps_ref, own_ref[...], inner_ref[...], outer_ref[...])
     gain = gain_ref[...]
     duals = duals_ref[...] + gain - fresh
     first, second = gaps(gain, fresh, fresh_ref[...])
@@ -265,20 +283,22 @@
 
     return pl.pallas_call(
         kernel,
-        out_shape=[jax.ShapeDtypeStruct(shape, F32) for shape in outs],
+        out_shape=[
+            jax.ShapeDtypeStruct(shape, F32) if isinstance(shape, tuple) else shape
+            for shape in outs
+        ],
         in_specs=[pl.BlockSpec(memory_space=space(i)) for i in range(len(ins))],
         out_specs=[pl.BlockSpec(memory_space=pltpu.VMEM) for _ in outs],
         scratch_shapes=scratch,
         cost_estimate=pl.CostEstimate(flops=flops, bytes_accessed=1000, transcendentals=0),
         compiler_params=pltpu.CompilerParams(vmem_limit_bytes=24 * 1024 * 1024),
-        name=kernel.__name__,
     )(*ins)
 
 
-def local(visibility, coherency, jones_start, duals_start):
+def solve(visibility, coherency, jones_start, duals_start):
     cards = lax.axis_size("chan")
     entries = jones_start.size * cards
-    odd = (lax.axis_index("chan") % 2).astype(jnp.int32).reshape(1)
+    card = lax.axis_index("chan").reshape(1)
     inner = [(i, i ^ 1) for i in range(cards)]
     outer = [(i, i - 1 if i % 2 == 0 else i + 1) for i in range(cards)]
     outer = [(a, b) for a, b in outer if 0 <= b < cards]
@@ -288,9 +308,17 @@
         pltpu.VMEM((2, GROUP * M, 256), F32),
         pltpu.VMEM((2, GROUP * 128, LANES), F32),
     ]
-    sums, gain, start, duals, ct, vt = call(
+    sums, gain, start, duals, taps, ct, vt = call(
         first_kernel,
-        [state, state, state, state, (2, ROWS, LANES), (2, ROWS, LANES)],
+        [
+            state,
+            state,
+            state,
+            state,
+            jax.ShapeDtypeStruct((6 * LANES, LANES), BF16),
+            (2, ROWS, LANES),
+            (2, ROWS, LANES),
+        ],
         (
             *(
                 pltpu.with_memory_space_constraint(x, pltpu.HBM)
@@ -298,6 +326,7 @@
                     coherency.reshape(2, 2, 16, 4, PAIRS), visibility, jones_start, duals_start
                 )
             ),
+            card,
         ),
         [
             pltpu.VMEM((2, 2, 16, 4, PAIRS), BF16),
@@ -312,11 +341,14 @@
             pltpu.SemaphoreType.DMA((7,)),
         ],
         hbm=(0, 1, 2, 3),
+        smem=(4,),
         flops=10**10,
     )
 
     def swapped(x):
-        return lax.ppermute(x, "chan", inner), lax.ppermute(x, "chan", outer)
+        far = lax.ppermute(x, "chan", outer)
+        near = lax.ppermute(x, "chan", inner)
+        return near, far
 
     near, far = swapped(sums)
     total, weight = call(
@@ -325,8 +357,7 @@
     sums, gain, fresh, duals, norms = call(
         third_kernel,
         [state, state, state, state, (1, LANES)],
-        (odd, sums, near, far, gain, start, duals, total, weight),
-        smem=(0,),
+        (taps, sums, near, far, gain, start, duals, total, weight),
     )
     near, far = swapped(sums)
     shape = jones_start.shape
@@ -334,8 +365,7 @@
     fresh, duals, norms = call(
         fourth_kernel,
         [state, state, (cards, 1, LANES)],
-        (odd, sums, near, far, gain, fresh, duals, norms),
-        smem=(0,),
+        (taps, sums, near, far, gain, fresh, duals, norms),
     )
     consensus, duals_now = call(turn_kernel, [shape, shape], (fresh, duals), flops=10**9)
     norms = lax.all_to_all(norms, "chan", split_axis=0, concat_axis=0, tiled=True)
@@ -351,7 +381,7 @@
         P(None, None, "slot", "chan", None),
     )
     return jax.shard_map(
-        local,
+        solve,
         mesh=mesh,
         in_specs=placed,
         out_specs=(

time: 46.1 us -> 45.7 us (level)
  no operation moved by 1% of the time
where the time goes in v3:
time: 45.7 us; the launch traced here: 45.5 us
  starting transfers between devices  21.5 us (47%)
  Pallas kernels  12 us (26%)
  waiting for transfers between devices  10.5 us (23%)
  between operations  0.7 us (2%)
  local copies, waits for them, and re-layouts  0.65 us (1%)
    all_to_all x1, starting transfers between devices, solve(): lax.all_to_all(norms, 'chan', split_axis=0, concat_axis=0, tiled=True)  12.9 us
    pallas_call x6, Pallas kernels, call(): pl.pallas_call(kernel, out_shape=[jax.ShapeDtypeStruct(shape, F32) if isi...  12 us
    all_to_all x1, waiting for transfers between devices, solve(): lax.all_to_all(norms, 'chan', split_axis=0, concat_axis=0, tiled=True)  8.51 us
    ppermute x2, starting transfers between devices, swapped(): far = lax.ppermute(x, 'chan', outer)  5.2 us
    ppermute x2, starting transfers between devices, swapped(): near = lax.ppermute(x, 'chan', inner)  3.38 us
    ppermute x2, waiting for transfers between devices, swapped(): far = lax.ppermute(x, 'chan', outer)  2 us
  transfers between devices with their start and end apart: 5, of which 3 were waited for; matrix products, arithmetic and copies ran while one was open for 0% of the time, Pallas kernels for 10%

profile of v3, /device:TPU:1, one launch (start us, length us, event | category | flops | bytes accessed | tf_op | source)
XLA Modules:
  0.0 45.5 jit_solution(9471012263572616354)
XLA Ops:
  0.6 5.9 %shard_map.75 = (f32[64,256]{1,0:T(8,128)S(1)}, f32[64,256]{1,0:T(8,128)S(1)}, f32[64,256]{1,0:T(8,128)S(1)}, f32[64,256]{1,0:T(8,128)S(1)}, bf16[768,128]{1,0:T...) custom-call(bf16[2,2,16,4,3844]{4,3,2,1,0:T(4,128)(2,1)} %bitcast.2, ...), custom_call_target="tpu_custom_call" | custom-call | flops 10000000000 | bytes 1000 | tf_op jit(solution)/shard_map/pallas_call | solution.py:284
  6.5 3.3 %collective-permute-start = (f32[64,256]{1,0:T(8,128)S(1)}, f32[64,256]{1,0:T(8,128)S(1)}, u32[]{:S(2)}, u32[]{:S(2)}) collective-permute-start(f32[64,256]{1,0:T(8,128)S(1)} %get-tuple-element.24.own_ref), channel_id=1, source_target_pairs={{0,4},{4,0},{8,12},{12,8},{16,20},{20,16},{24,28},{28,24},{32,36},... | collective-permute-start | bytes 196616 | tf_op jit(solution)/shard_map/ppermute | solution.py:350
  9.8 1.9 %collective-permute-start.1 = (f32[64,256]{1,0:T(8,128)S(1)}, f32[64,256]{1,0:T(8,128)S(1)}, u32[]{:S(2)}, u32[]{:S(2)}) collective-permute-start(f32[64,256]{1,0:T(8,128)S(1)} %get-tuple-element.24.own_ref), channel_id=1, source_target_pairs={{4,8},{8,4},{12,16},{16,12},{20,24},{24,20},{28,32},{32,28},{36,40... | collective-permute-start | bytes 196616 | tf_op jit(solution)/shard_map/ppermute | solution.py:349
  11.7 3.2 %shard_map.76 = (f32[64,256]{1,0:T(8,128)S(1)}, f32[64,128]{1,0:T(8,128)S(1)}) custom-call(f32[2,3968,128]{2,1,0:T(8,128)S(1)} %get-tuple-element.28.ct, f32[2,3968,128]{2,1,0:T(8,128)S(1)} %get-tuple-element.29.vt, f32[64,256]{1,0:T(8,128)S(1)} %get-tuple-element.25.gain_ref), custom_call_target="tpu_custom_call" | custom-call | flops 10000000000 | bytes 1000 | tf_op jit(solution)/shard_map/pallas_call | solution.py:284
  14.9 0.0 collective-permute-done.inner_ref
  14.9 0.5 %collective-permute-done.1.outer_ref = f32[64,256]{1,0:T(8,128)S(1)} collective-permute-done((f32[64,256]{1,0:T(8,128)S(1)}, f32[64,256]{1,0:T(8,128)S(1)}, u32[]{:S(2)}, u32[]{:S(2)}) %collective-permute-start.1) | collective-permute-done | bytes 65568 | tf_op jit(solution)/shard_map/ppermute | solution.py:349
  15.4 0.4 shard_map.77
  15.8 0.1 collective-permute-start.2
  15.9 3.3 %collective-permute-start.3 = (f32[64,256]{1,0:T(8,128)S(1)}, f32[64,256]{1,0:T(8,128)S(1)}, u32[]{:S(2)}, u32[]{:S(2)}) collective-permute-start(f32[64,256]{1,0:T(8,128)S(1)} %get-tuple-element.33.own_ref), channel_id=1, source_target_pairs={{4,8},{8,4},{12,16},{16,12},{20,24},{24,20},{28,32},{32,28},{36,40... | collective-permute-start | bytes 196616 | tf_op jit(solution)/shard_map/ppermute | solution.py:349
  19.2 0.8 %shard_map.78 = f32[2,2,16,4,62]{4,3,2,1,0:T(4,128)} custom-call(f32[64,256]{1,0:T(8,128)S(1)} %get-tuple-element.32.refs_0_.gain_ref), custom_call_target="tpu_custom_call" | custom-call | flops 1000000000 | bytes 1000 | tf_op jit(solution)/shard_map/pallas_call | solution.py:284
  19.9 0.0 collective-permute-done.2.inner_ref
  19.9 1.5 %collective-permute-done.3.outer_ref = f32[64,256]{1,0:T(8,128)S(1)} collective-permute-done((f32[64,256]{1,0:T(8,128)S(1)}, f32[64,256]{1,0:T(8,128)S(1)}, u32[]{:S(2)}, u32[]{:S(2)}) %collective-permute-start.3) | collective-permute-done | bytes 65568 | tf_op jit(solution)/shard_map/ppermute | solution.py:349
  21.5 1.0 %shard_map.79 = (f32[64,256]{1,0:T(8,128)S(1)}, f32[64,256]{1,0:T(8,128)S(1)}, f32[64,1,128]{2,1,0:T(1,128)}) custom-call(bf16[768,128]{1,0:T(8,128)(2,1)S(1)} %get-tuple-element.23.taps_ref, f32[64,256]{1,0:T(8,128)S(1)} %get-tuple-element.33.own_ref, f32[64,256]{1,0:T(8,128)S(1)} %collective-permute-done.2.inner_ref, ...), custom_call_target="tpu_custom_call" | custom-call | bytes 1000 | tf_op jit(solution)/shard_map/pallas_call | solution.py:284
  22.5 12.9 %all-to-all-start = ((f32[64,1,128]{2,1,0:T(1,128)}), f32[64,1,128]{2,1,0:T(1,128)S(1)}, u32[]{:S(2)}, u32[]{:S(2)}) async-start(f32[64,1,128]{2,1,0:T(1,128)} %get-tuple-element.41), calls=%async_computation | async-start | bytes 65536 | tf_op jit(solution)/shard_map/all_to_all | solution.py:371
  35.4 0.8 %shard_map.80 = (f32[2,2,16,4,62]{4,3,2,1,0:T(4,128)}, f32[2,2,16,4,62]{4,3,2,1,0:T(4,128)}) custom-call(f32[64,256]{1,0:T(8,128)S(1)} %get-tuple-element.37.refs_0_, f32[64,256]{1,0:T(8,128)S(1)} %get-tuple-element.38.refs_1_), custom_call_target="tpu_custom_call" | custom-call | flops 1000000000 | bytes 1000 | tf_op jit(solution)/shard_map/pallas_call | solution.py:284
  36.2 8.5 %all-to-all-done = f32[64,1,128]{2,1,0:T(1,128)S(1)} async-done(((f32[64,1,128]{2,1,0:T(1,128)}), f32[64,1,128]{2,1,0:T(1,128)S(1)}, u32[]{:S(2)}, u32[]{:S(2)}) %all-to-all-start) | async-done | bytes 32800 | tf_op jit(solution)/shard_map/all_to_all | solution.py:371
  44.7 0.1 slice_reduce_fusion
  44.8 0.6 %div.6 = f32[2,2]{1,0:T(2,128)} reshape(f32[4]{0:T(128)S(1)} %broadcast_multiply_fusion) | data formatting | bytes 32 | tf_op jit(solution)/shard_map/div | solution.py:372
  (1 shorter events, 0.0 us)
Async XLA Ops:
  6.5 8.4 %collective-permute-start = (f32[64,256]{1,0:T(8,128)S(1)}, f32[64,256]{1,0:T(8,128)S(1)}, u32[]{:S(2)}, u32[]{:S(2)}) collective-permute-start(f32[64,256]{1,0:T(8,128)S(1)} %get-tuple-element.24.own_ref), channel_id=1, source_target_pairs={{0,4},{4,0},{8,12},{12,8},{16,20},{20,16},{24,28},{28,24},{32,36},... | collective-permute-start | bytes 196616 | tf_op jit(solution)/shard_map/ppermute | solution.py:350
  9.8 5.6 %collective-permute-start.1 = (f32[64,256]{1,0:T(8,128)S(1)}, f32[64,256]{1,0:T(8,128)S(1)}, u32[]{:S(2)}, u32[]{:S(2)}) collective-permute-start(f32[64,256]{1,0:T(8,128)S(1)} %get-tuple-element.24.own_ref), channel_id=1, source_target_pairs={{4,8},{8,4},{12,16},{16,12},{20,24},{24,20},{28,32},{32,28},{36,40... | collective-permute-start | bytes 196616 | tf_op jit(solution)/shard_map/ppermute | solution.py:349
  15.8 4.2 %collective-permute-start.2 = (f32[64,256]{1,0:T(8,128)S(1)}, f32[64,256]{1,0:T(8,128)S(1)}, u32[]{:S(2)}, u32[]{:S(2)}) collective-permute-start(f32[64,256]{1,0:T(8,128)S(1)} %get-tuple-element.33.own_ref), channel_id=1, source_target_pairs={{0,4},{4,0},{8,12},{12,8},{16,20},{20,16},{24,28},{28,24},{32,36},... | collective-permute-start | bytes 196616 | tf_op jit(solution)/shard_map/ppermute | solution.py:350
  15.9 5.6 %collective-permute-start.3 = (f32[64,256]{1,0:T(8,128)S(1)}, f32[64,256]{1,0:T(8,128)S(1)}, u32[]{:S(2)}, u32[]{:S(2)}) collective-permute-start(f32[64,256]{1,0:T(8,128)S(1)} %get-tuple-element.33.own_ref), channel_id=1, source_target_pairs={{4,8},{8,4},{12,16},{16,12},{20,24},{24,20},{28,32},{32,28},{36,40... | collective-permute-start | bytes 196616 | tf_op jit(solution)/shard_map/ppermute | solution.py:349
  22.5 22.3 %all-to-all-start = ((f32[64,1,128]{2,1,0:T(1,128)}), f32[64,1,128]{2,1,0:T(1,128)S(1)}, u32[]{:S(2)}, u32[]{:S(2)}) async-start(f32[64,1,128]{2,1,0:T(1,128)} %get-tuple-element.41), calls=%async_computation | async-start | bytes 65536 | tf_op jit(solution)/shard_map/all_to_all | solution.py:371

commit v4 on v3

--- a/solution.py
+++ b/solution.py
@@ -67,12 +67,6 @@
         & (source % 4 == target % 4)
     )
     spread = jnp.where(spread, 1.0, 0.0).astype(BF16)
-    for start in range(0, ROWS, ROWS // 4):
-        wide = jnp.dot(
-            short[start : start + ROWS // 4], spread, preferred_element_type=F32
-        )
-        vt[0, start : start + ROWS // 4] = wide[:, :LANES]
-        vt[1, start : start + ROWS // 4] = wide[:, LANES:]
     for part in range(2):
         copies[1 + part * 2].wait()
         copies[2 + part * 2].wait()
@@ -91,18 +85,30 @@
         for p in range(N):
             ct[part, p * N + p : p * N + p + 1] = jnp.zeros((1, LANES), F32)
 
-
-def pair_sums(ct, vt, gain, total, weight, lhs, half, model):
+    def widen(start):
+        wide = jnp.dot(short[start : start + LANES], spread, preferred_element_type=F32)
+        vt[0, start : start + LANES] = wide[:, :LANES]
+        vt[1, start : start + LANES] = wide[:, LANES:]
+
+    return widen
+
+
+def pair_sums(ct, vt, gain, total, weight, lhs, half, model, widen=None):
     row = iota((256, LANES), 0) % LANES
     col = iota((256, LANES), 1)
     same = (row // 64 == col // 64) & (row % 4 == col % 4)
-    adder = jnp.where(same, 1.0, 0.0).astype(BF16)
+    adder = jnp.where(same, 1.0, 0.0)
 
     def count(group):
         return min(GROUP, N - group * GROUP)
 
+    ready = [0]
+
     def front(group):
         slot = group % 2
+        while widen and ready[0] < min((group * GROUP + count(group) - 1) * N + M, ROWS):
+            widen(ready[0])
+            ready[0] += LANES
         for i in range(count(group)):
             p = group * GROUP + i
             c_real = ct[0, p * N : p * N + M]
@@ -120,10 +126,12 @@
                 (i * 128 + M, p_real * h_imag + p_imag * h_real),
             ):
                 high = m.astype(BF16)
-                lhs[slot, at : at + M, :LANES] = high
-                lhs[slot, at : at + M, LANES:] = (m - high.astype(F32)).astype(BF16)
+                lhs[slot, at : at + M, :LANES] = m
+                lhs[slot, at : at + M, LANES:] = m - high.astype(F32)
         rows = count(group) * 128
-        model[slot, :rows] = jnp.dot(lhs[slot, :rows], adder, preferred_element_type=F32)
+        model[slot, :rows] = jnp.dot(
+            lhs[slot, :rows], adder, precision=lax.Precision.DEFAULT, preferred_element_type=F32
+        )
 
     def back(group):
         slot = group % 2
@@ -201,8 +209,8 @@
     start_ref[...] = rows_first(jones_ref)
     copies[1].wait()
     duals_out[...] = rows_first(duals_ref)
-    lay_out(coh_ref, vis_ref, vflat, short, ct, vt, copies[2:])
-    pair_sums(ct, vt, start_ref, total, weight, lhs, half, model)
+    widen = lay_out(coh_ref, vis_ref, vflat, short, ct, vt, copies[2:])
+    pair_sums(ct, vt, start_ref, total, weight, lhs, half, model, widen)
     gain = solved(total[...], weight[...], start_ref[...], start_ref[...] - duals_out[...])
     gain_ref[...] = gain
     sum_ref[...] = gain + duals_out[...]
@@ -304,7 +312,7 @@
     outer = [(a, b) for a, b in outer if 0 <= b < cards]
     state = (M, 2 * LANES)
     work = [
-        pltpu.VMEM((2, GROUP * 128, 256), BF16),
+        pltpu.VMEM((2, GROUP * 128, 256), F32),
         pltpu.VMEM((2, GROUP * M, 256), F32),
         pltpu.VMEM((2, GROUP * 128, LANES), F32),
     ]

time: 45.7 us -> 44.7 us (0.978)
  Pallas kernels: 12 us -> 10.4 us
  waiting for transfers between devices: 10.5 us -> 11.8 us
  starting transfers between devices: 21.5 us -> 20.9 us
    pallas_call x6, Pallas kernels: 12 us -> 10.4 us  [call(): pl.pallas_call(kernel, out_shape=[jax.ShapeDtypeStruct(shape, F32) if isi...]
    ppermute x2, waiting for transfers between devices: 2 us -> 3.29 us  [swapped(): far = lax.ppermute(x, 'chan', outer)]
    ppermute x2, starting transfers between devices: 5.2 us -> 4.55 us  [swapped(): far = lax.ppermute(x, 'chan', outer)]
  transfers between devices with their start and end apart: 5 -> 5, of which waited for: 3 -> 3; matrix products, arithmetic and copies ran while one was open for 0% -> 0% of each run, Pallas kernels for 10% -> 9%
where the time goes in v4:
time: 44.7 us; the launch traced here: 44.5 us
  starting transfers between devices  20.9 us (47%)
  waiting for transfers between devices  11.8 us (26%)
  Pallas kernels  10.4 us (23%)
  between operations  0.7 us (2%)
  local copies, waits for them, and re-layouts  0.65 us (1%)
    all_to_all x1, starting transfers between devices, solve(): lax.all_to_all(norms, 'chan', split_axis=0, concat_axis=0, tiled=True)  12.9 us
    pallas_call x6, Pallas kernels, call(): pl.pallas_call(kernel, out_shape=[jax.ShapeDtypeStruct(shape, F32) if isi...  10.4 us
    all_to_all x1, waiting for transfers between devices, solve(): lax.all_to_all(norms, 'chan', split_axis=0, concat_axis=0, tiled=True)  8.51 us
    ppermute x2, starting transfers between devices, swapped(): far = lax.ppermute(x, 'chan', outer)  4.55 us
    ppermute x2, starting transfers between devices, swapped(): near = lax.ppermute(x, 'chan', inner)  3.38 us
    ppermute x2, waiting for transfers between devices, swapped(): far = lax.ppermute(x, 'chan', outer)  3.29 us
  transfers between devices with their start and end apart: 5, of which 3 were waited for; matrix products, arithmetic and copies ran while one was open for 0% of the time, Pallas kernels for 9%

profile of v4, /device:TPU:1, one launch (start us, length us, event | category | flops | bytes accessed | tf_op | source)
XLA Modules:
  0.0 44.5 jit_solution(6458638686972245144)
XLA Ops:
  0.6 4.9 %shard_map.75 = (f32[64,256]{1,0:T(8,128)S(1)}, f32[64,256]{1,0:T(8,128)S(1)}, f32[64,256]{1,0:T(8,128)S(1)}, f32[64,256]{1,0:T(8,128)S(1)}, bf16[768,128]{1,0:T...) custom-call(bf16[2,2,16,4,3844]{4,3,2,1,0:T(4,128)(2,1)} %bitcast.2, ...), custom_call_target="tpu_custom_call" | custom-call | flops 10000000000 | bytes 1000 | tf_op jit(solution)/shard_map/pallas_call | solution.py:292
  5.6 3.3 %collective-permute-start = (f32[64,256]{1,0:T(8,128)S(1)}, f32[64,256]{1,0:T(8,128)S(1)}, u32[]{:S(2)}, u32[]{:S(2)}) collective-permute-start(f32[64,256]{1,0:T(8,128)S(1)} %get-tuple-element.24.own_ref), channel_id=1, source_target_pairs={{0,4},{4,0},{8,12},{12,8},{16,20},{20,16},{24,28},{28,24},{32,36},... | collective-permute-start | bytes 196616 | tf_op jit(solution)/shard_map/ppermute | solution.py:358
  8.9 1.9 %collective-permute-start.1 = (f32[64,256]{1,0:T(8,128)S(1)}, f32[64,256]{1,0:T(8,128)S(1)}, u32[]{:S(2)}, u32[]{:S(2)}) collective-permute-start(f32[64,256]{1,0:T(8,128)S(1)} %get-tuple-element.24.own_ref), channel_id=1, source_target_pairs={{4,8},{8,4},{12,16},{16,12},{20,24},{24,20},{28,32},{32,28},{36,40... | collective-permute-start | bytes 196616 | tf_op jit(solution)/shard_map/ppermute | solution.py:357
  10.8 2.5 %shard_map.76 = (f32[64,256]{1,0:T(8,128)S(1)}, f32[64,128]{1,0:T(8,128)S(1)}) custom-call(f32[2,3968,128]{2,1,0:T(8,128)S(1)} %get-tuple-element.28.ct, f32[2,3968,128]{2,1,0:T(8,128)S(1)} %get-tuple-element.29.vt, f32[64,256]{1,0:T(8,128)S(1)} %get-tuple-element.25.gain_ref), custom_call_target="tpu_custom_call" | custom-call | flops 10000000000 | bytes 1000 | tf_op jit(solution)/shard_map/pallas_call | solution.py:292
  13.3 0.0 collective-permute-done.inner_ref
  13.3 1.1 %collective-permute-done.1.outer_ref = f32[64,256]{1,0:T(8,128)S(1)} collective-permute-done((f32[64,256]{1,0:T(8,128)S(1)}, f32[64,256]{1,0:T(8,128)S(1)}, u32[]{:S(2)}, u32[]{:S(2)}) %collective-permute-start.1) | collective-permute-done | bytes 65568 | tf_op jit(solution)/shard_map/ppermute | solution.py:357
  14.4 0.4 shard_map.77
  14.8 0.1 collective-permute-start.2
  14.9 2.6 %collective-permute-start.3 = (f32[64,256]{1,0:T(8,128)S(1)}, f32[64,256]{1,0:T(8,128)S(1)}, u32[]{:S(2)}, u32[]{:S(2)}) collective-permute-start(f32[64,256]{1,0:T(8,128)S(1)} %get-tuple-element.33.own_ref), channel_id=1, source_target_pairs={{4,8},{8,4},{12,16},{16,12},{20,24},{24,20},{28,32},{32,28},{36,40... | collective-permute-start | bytes 196616 | tf_op jit(solution)/shard_map/ppermute | solution.py:357
  17.6 0.8 %shard_map.78 = f32[2,2,16,4,62]{4,3,2,1,0:T(4,128)} custom-call(f32[64,256]{1,0:T(8,128)S(1)} %get-tuple-element.32.refs_0_.gain_ref), custom_call_target="tpu_custom_call" | custom-call | flops 1000000000 | bytes 1000 | tf_op jit(solution)/shard_map/pallas_call | solution.py:292
  18.3 0.0 collective-permute-done.2.inner_ref
  18.3 2.2 %collective-permute-done.3.outer_ref = f32[64,256]{1,0:T(8,128)S(1)} collective-permute-done((f32[64,256]{1,0:T(8,128)S(1)}, f32[64,256]{1,0:T(8,128)S(1)}, u32[]{:S(2)}, u32[]{:S(2)}) %collective-permute-start.3) | collective-permute-done | bytes 65568 | tf_op jit(solution)/shard_map/ppermute | solution.py:357
  20.5 1.0 %shard_map.79 = (f32[64,256]{1,0:T(8,128)S(1)}, f32[64,256]{1,0:T(8,128)S(1)}, f32[64,1,128]{2,1,0:T(1,128)}) custom-call(bf16[768,128]{1,0:T(8,128)(2,1)S(1)} %get-tuple-element.23.taps_ref, f32[64,256]{1,0:T(8,128)S(1)} %get-tuple-element.33.own_ref, f32[64,256]{1,0:T(8,128)S(1)} %collective-permute-done.2.inner_ref, ...), custom_call_target="tpu_custom_call" | custom-call | bytes 1000 | tf_op jit(solution)/shard_map/pallas_call | solution.py:292
  21.5 12.9 %all-to-all-start = ((f32[64,1,128]{2,1,0:T(1,128)}), f32[64,1,128]{2,1,0:T(1,128)S(1)}, u32[]{:S(2)}, u32[]{:S(2)}) async-start(f32[64,1,128]{2,1,0:T(1,128)} %get-tuple-element.41), calls=%async_computation | async-start | bytes 65536 | tf_op jit(solution)/shard_map/all_to_all | solution.py:379
  34.5 0.8 %shard_map.80 = (f32[2,2,16,4,62]{4,3,2,1,0:T(4,128)}, f32[2,2,16,4,62]{4,3,2,1,0:T(4,128)}) custom-call(f32[64,256]{1,0:T(8,128)S(1)} %get-tuple-element.37.refs_0_, f32[64,256]{1,0:T(8,128)S(1)} %get-tuple-element.38.refs_1_), custom_call_target="tpu_custom_call" | custom-call | flops 1000000000 | bytes 1000 | tf_op jit(solution)/shard_map/pallas_call | solution.py:292
  35.3 8.5 %all-to-all-done = f32[64,1,128]{2,1,0:T(1,128)S(1)} async-done(((f32[64,1,128]{2,1,0:T(1,128)}), f32[64,1,128]{2,1,0:T(1,128)S(1)}, u32[]{:S(2)}, u32[]{:S(2)}) %all-to-all-start) | async-done | bytes 32800 | tf_op jit(solution)/shard_map/all_to_all | solution.py:379
  43.8 0.1 slice_reduce_fusion
  43.9 0.6 %div.6 = f32[2,2]{1,0:T(2,128)} reshape(f32[4]{0:T(128)S(1)} %broadcast_multiply_fusion) | data formatting | bytes 32 | tf_op jit(solution)/shard_map/div | solution.py:380
  (1 shorter events, 0.0 us)
Async XLA Ops:
  5.6 7.7 %collective-permute-start = (f32[64,256]{1,0:T(8,128)S(1)}, f32[64,256]{1,0:T(8,128)S(1)}, u32[]{:S(2)}, u32[]{:S(2)}) collective-permute-start(f32[64,256]{1,0:T(8,128)S(1)} %get-tuple-element.24.own_ref), channel_id=1, source_target_pairs={{0,4},{4,0},{8,12},{12,8},{16,20},{20,16},{24,28},{28,24},{32,36},... | collective-permute-start | bytes 196616 | tf_op jit(solution)/shard_map/ppermute | solution.py:358
  8.9 5.6 %collective-permute-start.1 = (f32[64,256]{1,0:T(8,128)S(1)}, f32[64,256]{1,0:T(8,128)S(1)}, u32[]{:S(2)}, u32[]{:S(2)}) collective-permute-start(f32[64,256]{1,0:T(8,128)S(1)} %get-tuple-element.24.own_ref), channel_id=1, source_target_pairs={{4,8},{8,4},{12,16},{16,12},{20,24},{24,20},{28,32},{32,28},{36,40... | collective-permute-start | bytes 196616 | tf_op jit(solution)/shard_map/ppermute | solution.py:357
  14.8 3.5 %collective-permute-start.2 = (f32[64,256]{1,0:T(8,128)S(1)}, f32[64,256]{1,0:T(8,128)S(1)}, u32[]{:S(2)}, u32[]{:S(2)}) collective-permute-start(f32[64,256]{1,0:T(8,128)S(1)} %get-tuple-element.33.own_ref), channel_id=1, source_target_pairs={{0,4},{4,0},{8,12},{12,8},{16,20},{20,16},{24,28},{28,24},{32,36},... | collective-permute-start | bytes 196616 | tf_op jit(solution)/shard_map/ppermute | solution.py:358
  14.9 5.6 %collective-permute-start.3 = (f32[64,256]{1,0:T(8,128)S(1)}, f32[64,256]{1,0:T(8,128)S(1)}, u32[]{:S(2)}, u32[]{:S(2)}) collective-permute-start(f32[64,256]{1,0:T(8,128)S(1)} %get-tuple-element.33.own_ref), channel_id=1, source_target_pairs={{4,8},{8,4},{12,16},{16,12},{20,24},{24,20},{28,32},{32,28},{36,40... | collective-permute-start | bytes 196616 | tf_op jit(solution)/shard_map/ppermute | solution.py:357
  21.5 22.3 %all-to-all-start = ((f32[64,1,128]{2,1,0:T(1,128)}), f32[64,1,128]{2,1,0:T(1,128)S(1)}, u32[]{:S(2)}, u32[]{:S(2)}) async-start(f32[64,1,128]{2,1,0:T(1,128)} %get-tuple-element.41), calls=%async_computation | async-start | bytes 65536 | tf_op jit(solution)/shard_map/all_to_all | solution.py:379
